TPU v7x, 512 devices: a whole 4x8x8 slice. The times are simulated.
512 devices in a mesh: batch: 8 (over y_lo, x), rows: 8 (over z), chan: 8 (over y_hi, core).
Axes of the slice: x: 4, y: 8 (y_hi: 4, y_lo: 2; y = y_hi * 2 + y_lo), z: 8, core: 2. Of those that a mesh axis runs over, the one named last changes fastest.
Arguments:
- images: float32 [64, 24, 64, 32], P('batch', None, ('rows', 'chan')), may hold values from -6 to 6
- shift_mid: float32 [3, 24], replicated, may hold values from -1.75 to 1.75
- gain_mid: float32 [3, 24], replicated, may hold values from -0.3 to 0.3
- lower_mid: float32 [3, 24, 24], replicated, may hold values from -1.25 to 1.25
- upper_mid: float32 [3, 24, 24], replicated, may hold values from -1.25 to 1.25
- diag_mid: float32 [3, 24], replicated, may hold values from -0.3 to 0.3
- first_mid: bfloat16 [3, 9, 12, 512], replicated, may hold values from -0.625 to 0.625
- first_bias_mid: bfloat16 [3, 512], replicated, may hold values from -3 to 3
- second_mid: bfloat16 [3, 512, 512], replicated, may hold values from -0.25 to 0.25
- second_bias_mid: float32 [3, 512], replicated, may hold values from -3 to 3
- third_mid: bfloat16 [3, 9, 512, 24], replicated, may hold values from -0.09375 to 0.09375
- third_bias_mid: float32 [3, 24], replicated, may hold values from -3 to 3
- shift_top: float32 [2, 48], replicated, may hold values from -1.75 to 1.75
- gain_top: float32 [2, 48], replicated, may hold values from -0.3 to 0.3
- lower_top: float32 [2, 48, 48], replicated, may hold values from -0.875 to 0.875
- upper_top: float32 [2, 48, 48], replicated, may hold values from -0.875 to 0.875
- diag_top: float32 [2, 48], replicated, may hold values from -0.3 to 0.3
- first_top: bfloat16 [2, 9, 24, 512], replicated, may hold values from -0.4375 to 0.4375
- first_bias_top: bfloat16 [2, 512], replicated, may hold values from -3 to 3
- second_top: bfloat16 [2, 512, 512], replicated, may hold values from -0.25 to 0.25
- second_bias_top: float32 [2, 512], replicated, may hold values from -3 to 3
- third_top: bfloat16 [2, 9, 512, 48], replicated, may hold values from -0.09375 to 0.09375
- third_bias_top: float32 [2, 48], replicated, may hold values from -3 to 3
Outputs:
- latent_mid: float32 [64, 12, 64, 32], P('batch', None, ('rows', 'chan'))
- latent_top: float32 [64, 48, 32, 16], P(('batch', 'chan'), None, 'rows')
- loglik: float32 [64], P(('batch', 'chan'))
All inputs are finite; a program needn't handle non-finite values.
Results may differ from a plain program's by a relative error of at most 0.008.
Values may be sent and summed in bfloat16 or wider, within the bound.
A program may use at most 64 MiB of HBM per device.

v0:
```python
import functools
import math

import jax
import jax.numpy as jnp
from jax import lax
from jax.experimental import pallas as pl
from jax.experimental.pallas import tpu as pltpu
from jax.sharding import PartitionSpec as P

MESH = pl.DeviceIdType.MESH
LANES = 128
CHUNK = 256
FINE = lax.Precision.HIGHEST
log_two_pi = math.log(2.0 * math.pi)
f32 = jnp.float32
bf16 = jnp.bfloat16


def up8(n):
    return -(-n // 8) * 8


def iota(shape, dim):
    return lax.broadcasted_iota(jnp.int32, shape, dim)


def dot_nt(a, b, precision=None):
    return lax.dot_general(
        a, b, (((1,), (1,)), ((), ())), preferred_element_type=f32, precision=precision
    )


def dot_tn(a, b):
    return lax.dot_general(a, b, (((0,), (0,)), ((), ())), preferred_element_type=f32)


def roll_back(x, amount):
    n = x.shape[1]
    amount = amount % n
    return x if amount == 0 else pltpu.roll(x, n - amount, 1)


def neighbour_masks(n, height, width):
    lane = iota((1, n), 1)
    place = lax.rem(lane, height * width)
    row = lax.div(place, width)
    col = lax.rem(place, width)
    row_ok = {-1: row >= 1, 1: row < height - 1}
    col_ok = {-1: col >= 1, 1: col < width - 1}
    return row_ok, col_ok


def keep(x, ok):
    return jnp.where(ok, x, 0.0)


def spread_taps(q, masks, width):
    row_ok, col_ok = masks
    by_col = {}
    for dc in (-1, 0, 1):
        by_col[dc] = q if dc == 0 else keep(roll_back(q, dc), col_ok[dc])
    taps = []
    for dr in (-1, 0, 1):
        for dc in (-1, 0, 1):
            x = by_col[dc]
            taps.append(x if dr == 0 else keep(roll_back(x, dr * width), row_ok[dr]))
    return jnp.concatenate(taps, axis=0)


def gather_taps(y_ref, channels, n, masks, width):
    row_ok, col_ok = masks
    total = None
    for dc in (-1, 0, 1):
        part = None
        for dr in (-1, 0, 1):
            tap = (dr + 1) * 3 + dc + 1
            y = y_ref[tap * channels : (tap + 1) * channels, :n]
            if dr != 0:
                y = keep(roll_back(y, dr * width), row_ok[dr])
            part = y if part is None else part + y
        if dc != 0:
            part = keep(roll_back(part, dc), col_ok[dc])
        total = part if total is None else total + part
    return total


def mixing(lower, upper, diag_row, gain_row, shift_row, in_map):
    channels = lower.shape[0]
    half = channels // 2
    padded = up8(half)
    i = iota((channels, channels), 0)
    j = iota((channels, channels), 1)
    eye = jnp.where(i == j, 1.0, 0.0)
    low = jnp.where(i > j, lower, 0.0) + eye
    upp = (jnp.where(i < j, upper, 0.0) + eye * jnp.exp(diag_row)) * jnp.exp(gain_row)
    out_map = pad_map(channels)
    rows = jnp.dot(out_map, low, precision=FINE, preferred_element_type=f32)
    mat = jnp.dot(rows, upp, precision=FINE, preferred_element_type=f32)
    bias = jnp.sum(mat * shift_row, axis=1, keepdims=True)
    if in_map is not None:
        mat = dot_nt(mat, in_map, FINE)
    return mat, bias


def pad_map(channels):
    half = channels // 2
    padded = up8(half)
    i = iota((2 * padded, channels), 0)
    j = iota((2 * padded, channels), 1)
    first = (j < half) & (i == j)
    second = (j >= half) & (i - padded == j - half)
    return jnp.where(first | second, 1.0, 0.0)


def squeeze_map(kept, padded):
    i = iota((4 * padded, 4 * kept), 0)
    j = iota((4 * padded, 4 * kept), 1)
    same = (lax.rem(i, padded) == lax.div(j, 4)) & (lax.div(i, padded) == lax.rem(j, 4))
    return jnp.where(same, 1.0, 0.0)


def to_column(row):
    n = row.shape[1]
    eye = iota((n, n), 0) == iota((n, n), 1)
    return jnp.sum(jnp.where(eye, row, 0.0), axis=1, keepdims=True)


def kernel(dims, *refs):
    count = dims[-1]
    sources, refs = refs[:count], refs[count:]
    (mid_out, top_out, lik_out), refs = refs[:3], refs[3:]
    held, refs = refs[:count], refs[count:]
    (
        images,
        shift_mid,
        gain_mid,
        lower_mid,
        upper_mid,
        diag_mid,
        w1_raw,
        first_bias_mid,
        w2_mid,
        second_bias_mid,
        w3_mid,
        third_bias_mid,
        shift_top,
        gain_top,
        lower_top,
        upper_top,
        diag_top,
        w1_top,
        first_bias_top,
        w2_top,
        second_bias_top,
        w3_top,
        third_bias_top,
    ) = held
    (
        outbox,
        inbox,
        w1_mid,
        pick,
        y_scr,
        z_scr,
        z_send,
        z_recv,
        w_sem,
        send_sem,
        recv_sem,
        z_send_sem,
        z_recv_sem,
        t_send,
        t_recv,
        t_send_sem,
        t_recv_sem,
    ) = refs
    n_rows, n_chan, split, height, width, _ = dims
    n_imgs, channels, block = images.shape
    steps_mid = shift_mid.shape[0]
    steps_top = shift_top.shape[0]
    group = n_imgs // n_chan
    peers = n_rows * n_chan
    b = lax.axis_index("batch")
    r = lax.axis_index("rows")
    c = lax.axis_index("chan")
    me = r * n_chan + c
    mine = lax.rem(r, split)
    base = r - mine
    own_imgs = group // split

    def device(row, chan):
        return {"batch": b, "rows": row, "chan": chan}

    barrier = pltpu.get_barrier_semaphore()
    for d in range(1, peers):
        other = lax.rem(me + d, peers)
        pl.semaphore_signal(
            barrier,
            inc=1,
            device_id=device(other // n_chan, lax.rem(other, n_chan)),
            device_id_type=MESH,
        )

    copies = []
    for at in range(count):
        copy = pltpu.make_async_copy(sources[at], held[at], w_sem.at[at])
        copy.start()
        copies.append(copy)
    copies[0].wait()

    per = LANES // block
    slabs = channels // 8
    pieces = [(img, slab) for img in range(own_imgs) for slab in range(slabs)]
    packs = -(-len(pieces) // per)
    for dest in range(n_chan * split):
        rows = []
        for pack in range(packs):
            parts = []
            for img, slab in pieces[pack * per : (pack + 1) * per]:
                parts.append(images[dest * own_imgs + img, slab * 8 : slab * 8 + 8, :])
            while len(parts) < per:
                parts.append(jnp.zeros((8, block), f32))
            rows.append(jnp.concatenate(parts, axis=1))
        outbox[dest] = jnp.concatenate(rows, axis=0).astype(bf16)

    pl.semaphore_wait(barrier, peers - 1)
    sends = []
    for d in range(1, peers):
        other = lax.rem(me + d, peers)
        other_chan = lax.rem(other, n_chan)
        copy = pltpu.make_async_remote_copy(
            src_ref=outbox.at[other_chan * split + lax.rem(other // n_chan, split)],
            dst_ref=inbox.at[me],
            send_sem=send_sem.at[d],
            recv_sem=recv_sem.at[d],
            device_id=device(other // n_chan, other_chan),
            device_id_type=MESH,
        )
        copy.start()
        sends.append(copy)

    inbox[me] = outbox[c * split + mine]

    for copy in copies[1:]:
        copy.wait()
    half = channels // 2
    padded = up8(half)
    top_channels = 4 * half
    mats_mid = []
    for s in range(steps_mid):
        mats_mid.append(
            mixing(
                lower_mid[s],
                upper_mid[s],
                diag_mid[s : s + 1, :],
                gain_mid[s : s + 1, :],
                shift_mid[s : s + 1, :],
                None if s == 0 else pad_map(channels),
            )
        )
    mats_top = []
    for s in range(steps_top):
        mats_top.append(
            mixing(
                lower_top[s],
                upper_top[s],
                diag_top[s : s + 1, :],
                gain_top[s : s + 1, :],
                shift_top[s : s + 1, :],
                squeeze_map(half, padded) if s == 0 else pad_map(top_channels),
            )
        )
    bias3_mid = [to_column(third_bias_mid[s : s + 1, :]) for s in range(steps_mid)]
    bias3_top = [to_column(third_bias_top[s : s + 1, :]) for s in range(steps_top)]
    span = pick.shape[0]
    quarter = span // 4
    to = iota((1, span), 1)
    ij = lax.div(to, quarter)
    cell = lax.rem(to, quarter)
    coarse_w = width // 2
    origin = (2 * lax.div(cell, coarse_w) + lax.div(ij, 2)) * width
    origin = origin + 2 * lax.rem(cell, coarse_w) + lax.rem(ij, 2)
    for k in range(0, span, LANES):
        pick[k : k + LANES, :] = jnp.where(
            iota((LANES, span), 0) + k == origin, 1.0, 0.0
        ).astype(bf16)
    for s in range(steps_mid):
        for tap in range(9):
            w = w1_raw[s, tap].astype(f32)
            if padded > half:
                w = jnp.concatenate([w, jnp.zeros((padded - half, w.shape[1]), f32)], axis=0)
            w1_mid[s, tap * padded : (tap + 1) * padded, :] = w.astype(bf16)
    const_mid = height * width * (jnp.sum(gain_mid[...]) + jnp.sum(diag_mid[...]))
    const_top = (height // 2) * (width // 2) * (jnp.sum(gain_top[...]) + jnp.sum(diag_top[...]))

    for d in range(1, peers):
        source = lax.rem(me + peers - d, peers)
        pltpu.make_async_remote_copy(
            src_ref=outbox.at[0],
            dst_ref=inbox.at[source],
            send_sem=send_sem.at[d],
            recv_sem=recv_sem.at[d],
            device_id=device(r, c),
            device_id_type=MESH,
        ).wait_recv()

    cells = height * width
    n_mid = own_imgs * cells
    columns = []
    letters = [inbox[source].astype(f32) for source in range(peers)]
    for img in range(own_imgs):
        for quad in range(peers // per):
            stack = []
            for slab in range(slabs):
                at = img * slabs + slab
                lo = (at % per) * block
                top = at // per * 8
                parts = [
                    letters[quad * per + j][top : top + 8, lo : lo + block] for j in range(per)
                ]
                stack.append(jnp.concatenate(parts, axis=1))
            columns.append(jnp.concatenate(stack, axis=0))
    state = jnp.concatenate(columns, axis=1)

    def step(state, mat, bias, w1, b1, w2, b2, w3, b3, masks, width, chans):
        n = state.shape[1]
        half_c = chans // 2
        hp = up8(half_c)
        u = jnp.dot(mat, state, precision=FINE, preferred_element_type=f32) + bias
        ua, ub = u[:hp], u[hp:]
        spread = spread_taps(ua, masks, width).astype(bf16)
        size = min(CHUNK, n)
        for at in range(0, n, size):
            h1 = dot_tn(spread[:, at : at + size], w1)
            h1 = jnp.maximum(h1 + b1, 0.0).astype(bf16)
            h2 = jnp.dot(h1, w2[...], preferred_element_type=f32)
            h2 = jnp.maximum(h2 + b2, 0.0).astype(bf16)
            y_scr[: 9 * chans, at : at + size] = dot_nt(w3[...], h2)
        out = gather_taps(y_scr, chans, n, masks, width) + b3
        g = out[:hp] + 2.0
        t = out[half_c:]
        if hp > half_c:
            t = jnp.concatenate([t, jnp.zeros((hp - half_c, n), f32)], axis=0)
        e = jnp.exp(-jnp.abs(g))
        inv = 1.0 / (1.0 + e)
        gate = jnp.where(g >= 0, inv, e * inv)
        logs = jnp.minimum(g, 0.0) - jnp.log(1.0 + e)
        if hp > half_c:
            logs = jnp.where(iota((hp, n), 0) < half_c, logs, 0.0)
        return ua, (ub + t) * gate, logs

    masks = neighbour_masks(n_mid, height, width)
    score = None
    for s in range(steps_mid):
        ua, updated, logs = step(
            state,
            *mats_mid[s],
            w1_mid[s],
            first_bias_mid[s : s + 1, :].astype(f32),
            w2_mid.at[s],
            second_bias_mid[s : s + 1, :],
            w3_mid.at[s],
            bias3_mid[s],
            masks,
            width,
            channels,
        )
        score = logs if score is None else score + logs
        if s < steps_mid - 1:
            state = jnp.concatenate([ua, updated], axis=0)
    score = score - 0.5 * ua * ua
    z_scr[...] = ua
    strip = n_chan * block
    for to_row in range(split):
        for img in range(own_imgs):
            begin = pl.multiple_of(img * cells + (base + to_row) * strip, LANES)
            z_send[to_row, img] = z_scr[:, pl.ds(begin, strip)]

    parts = []
    rest = updated
    for _ in range(3):
        piece = rest.astype(bf16)
        rest = rest - piece.astype(f32)
        parts.append(piece)
    blocks = []
    parts = jnp.concatenate([x.astype(f32) for x in parts], axis=0).astype(bf16)
    for at in range(0, n_mid, span):
        got = jnp.dot(parts[:, at : at + span], pick[...], preferred_element_type=f32)
        total = got[:padded] + got[padded : 2 * padded] + got[2 * padded :]
        blocks.append(
            jnp.concatenate([total[:, k * quarter : (k + 1) * quarter] for k in range(4)], axis=0)
        )
    state = jnp.concatenate(blocks, axis=1)

    team = split * n_chan
    seat = mine * n_chan + c
    z_copies = []
    for d in range(1, team):
        other = lax.rem(seat + d, team)
        copy = pltpu.make_async_remote_copy(
            src_ref=z_send.at[other // n_chan],
            dst_ref=z_recv.at[seat],
            send_sem=z_send_sem.at[d],
            recv_sem=z_recv_sem.at[d],
            device_id=device(base + other // n_chan, lax.rem(other, n_chan)),
            device_id_type=MESH,
        )
        copy.start()
        z_copies.append(copy)
    z_recv[seat] = z_send[mine]

    n_top = n_mid // 4
    masks = neighbour_masks(n_top, height // 2, width // 2)
    score_top = None
    for s in range(steps_top):
        ua, updated, logs = step(
            state,
            *mats_top[s],
            w1_top[s],
            first_bias_top[s : s + 1, :].astype(f32),
            w2_top.at[s],
            second_bias_top[s : s + 1, :],
            w3_top.at[s],
            bias3_top[s],
            masks,
            width // 2,
            top_channels,
        )
        score_top = logs if score_top is None else score_top + logs
        state = jnp.concatenate([ua, updated], axis=0)
    score_top = score_top - 0.5 * (ua * ua + updated * updated)

    top_cells = cells // 4
    own = top_cells // n_rows
    hp = up8(top_channels // 2)
    if hp * 2 > top_channels:
        state = jnp.concatenate([ua[: top_channels // 2], updated[: top_channels // 2]], axis=0)
    flipped = jnp.transpose(state)
    y_scr[: flipped.shape[0], :top_channels] = flipped
    for to_row in range(split):
        for img in range(own_imgs):
            begin = pl.multiple_of(img * top_cells + (base + to_row) * own, 8)
            t_send[to_row, img, :own, :] = y_scr[pl.ds(begin, own), :top_channels]
    fixed = const_mid + const_top - 0.5 * log_two_pi * (half * cells + top_channels * top_cells)
    for img in range(own_imgs):
        total = jnp.sum(score[:, img * cells : (img + 1) * cells])
        total = total + jnp.sum(score_top[:, img * top_cells : (img + 1) * top_cells])
        lik = jnp.full((8, top_channels), (total + fixed) / (channels * cells), f32)
        for to_row in range(split):
            t_send[to_row, img, own:, :] = lik
    t_copies = []
    for d in range(1, split):
        other = lax.rem(mine + d, split)
        copy = pltpu.make_async_remote_copy(
            src_ref=t_send.at[other],
            dst_ref=t_recv.at[mine],
            send_sem=t_send_sem.at[d],
            recv_sem=t_recv_sem.at[d],
            device_id=device(base + other, c),
            device_id_type=MESH,
        )
        copy.start()
        t_copies.append(copy)
    t_recv[mine] = t_send[mine]

    for d in range(1, team):
        pltpu.make_async_remote_copy(
            src_ref=z_send.at[0],
            dst_ref=z_recv.at[lax.rem(seat + team - d, team)],
            send_sem=z_send_sem.at[d],
            recv_sem=z_recv_sem.at[d],
            device_id=device(r, c),
            device_id_type=MESH,
        ).wait_recv()
    for here in range(n_chan):

        @pl.when(c == here)
        def _():
            for source in range(n_chan):
                for img in range(group):
                    sender = img // own_imgs * n_chan + source
                    mid_out[source * group + img] = z_recv[sender, img % own_imgs][
                        :half, here * block : (here + 1) * block
                    ]

    for copy in sends + z_copies:
        copy.wait_send()
    for d in range(1, split):
        pltpu.make_async_remote_copy(
            src_ref=t_send.at[0],
            dst_ref=t_recv.at[lax.rem(mine + split - d, split)],
            send_sem=t_send_sem.at[d],
            recv_sem=t_recv_sem.at[d],
            device_id=device(r, c),
            device_id_type=MESH,
        ).wait_recv()
    for copy in t_copies:
        copy.wait_send()
    for img in range(group):
        letter = t_recv[img // own_imgs, img % own_imgs]
        top_out[img] = letter[:own]
        lik_out[img] = jnp.max(letter[own:])


def deliver(mid, top, lik, mid_out, top_out, lik_out):
    width = mid_out.shape[3]
    for img in range(mid.shape[0]):
        for row in range(mid_out.shape[2]):
            mid_out[img, :, row, :] = mid[img][:, row * width : (row + 1) * width]
    top_out[...] = top[...]
    for img in range(lik.shape[0]):
        lik_out[img] = lik[img]


def body(sizes, images, *params):
    (
        shift_mid,
        gain_mid,
        lower_mid,
        upper_mid,
        diag_mid,
        first_mid,
        first_bias_mid,
        second_mid,
        second_bias_mid,
        third_mid,
        third_bias_mid,
        shift_top,
        gain_top,
        lower_top,
        upper_top,
        diag_top,
        first_top,
        first_bias_top,
        second_top,
        second_bias_top,
        third_top,
        third_bias_top,
    ) = params
    n_rows, n_chan = sizes
    n_imgs, channels, own_rows, width = images.shape
    peers = n_rows * n_chan
    height = own_rows * peers
    block = own_rows * width
    group = n_imgs // n_chan
    half = channels // 2
    padded = up8(half)
    steps_mid, hidden = first_bias_mid.shape
    steps_top, top_channels = shift_top.shape
    cells = height * width
    split = group if n_rows % group == 0 else 1
    own_imgs = group // split
    n_mid = own_imgs * cells
    span = 4 * LANES
    packs = -(-(own_imgs * (channels // 8)) * block // LANES)
    strip = n_chan * block
    own = cells // 4 // n_rows

    w1_top = first_top.reshape(steps_top, -1, hidden)
    w3_mid = third_mid.transpose(0, 1, 3, 2).reshape(steps_mid, -1, hidden)
    w3_top = third_top.transpose(0, 1, 3, 2).reshape(steps_top, -1, hidden)
    operands = (
        images.reshape(n_imgs, channels, block),
        shift_mid,
        gain_mid,
        lower_mid,
        upper_mid,
        diag_mid,
        first_mid,
        first_bias_mid,
        second_mid,
        second_bias_mid,
        w3_mid,
        third_bias_mid,
        shift_top,
        gain_top,
        lower_top,
        upper_top,
        diag_top,
        w1_top,
        first_bias_top,
        second_top,
        second_bias_top,
        w3_top,
        third_bias_top,
    )
    vmem = pl.BlockSpec(memory_space=pltpu.VMEM)
    smem = pl.BlockSpec(memory_space=pltpu.SMEM)
    count = len(operands)
    mid, top, lik = pl.pallas_call(
        functools.partial(kernel, (n_rows, n_chan, split, height, width, count)),
        out_shape=(
            jax.ShapeDtypeStruct((n_imgs, half, block), f32),
            jax.ShapeDtypeStruct((group, own, top_channels), f32),
            jax.ShapeDtypeStruct((group,), f32),
        ),
        in_specs=[pl.BlockSpec(memory_space=pl.ANY)] * count,
        out_specs=(vmem, vmem, smem),
        scratch_shapes=[pltpu.VMEM(x.shape, x.dtype) for x in operands]
        + [
            pltpu.VMEM((n_chan * split, packs * 8, LANES), bf16),
            pltpu.VMEM((peers, packs * 8, LANES), bf16),
            pltpu.VMEM((steps_mid, 9 * padded, hidden), bf16),
            pltpu.VMEM((span, span), bf16),
            pltpu.VMEM((max(9 * top_channels, n_mid // 4), n_mid), f32),
            pltpu.VMEM((padded, n_mid), f32),
            pltpu.VMEM((split, own_imgs, padded, strip), f32),
            pltpu.VMEM((split * n_chan, own_imgs, padded, strip), f32),
            pltpu.SemaphoreType.DMA((count,)),
            pltpu.SemaphoreType.DMA((peers,)),
            pltpu.SemaphoreType.DMA((peers,)),
            pltpu.SemaphoreType.DMA((split * n_chan,)),
            pltpu.SemaphoreType.DMA((split * n_chan,)),
            pltpu.VMEM((split, own_imgs, own + 8, top_channels), f32),
            pltpu.VMEM((split, own_imgs, own + 8, top_channels), f32),
            pltpu.SemaphoreType.DMA((split,)),
            pltpu.SemaphoreType.DMA((split,)),
        ],
        compiler_params=pltpu.CompilerParams(
            collective_id=0, has_side_effects=True, vmem_limit_bytes=56 * 1024 * 1024
        ),
        name="flow",
    )(*operands)
    latent_mid, top, lik = pl.pallas_call(
        deliver,
        out_shape=(
            jax.ShapeDtypeStruct((n_imgs, half, own_rows, width), f32),
            jax.ShapeDtypeStruct(top.shape, f32),
            jax.ShapeDtypeStruct(lik.shape, f32),
        ),
        in_specs=[vmem, vmem, smem],
        out_specs=(vmem, vmem, smem),
        name="deliver",
    )(mid, top, lik)
    latent_top = top.reshape(group, -1, width // 2, top_channels).transpose(0, 3, 1, 2)
    return latent_mid, latent_top, lik


def solution(mesh):
    sizes = (mesh.shape["rows"], mesh.shape["chan"])
    placed = (P("batch", None, ("rows", "chan"), None),) + (P(),) * 22
    return jax.shard_map(
        functools.partial(body, sizes),
        mesh=mesh,
        in_specs=placed,
        out_specs=(
            P("batch", None, ("rows", "chan"), None),
            P(("batch", "chan"), None, "rows", None),
            P(("batch", "chan")),
        ),
        check_vma=False,
    )
```

profile of v0, /device:TPU:1, one launch (start us, length us, event | category | flops | bytes accessed | tf_op | source)
XLA Modules:
  0.0 50.4 jit_solution(13425350760018961561)
XLA Ops:
  0.6 47.5 %flow.1 = (f32[8,12,32]{2,1,0:T(8,128)}, f32[1,64,48]{2,1,0:T(8,128)}, f32[1]{0:T(128)}) custom-call(f32[8,24,32]{2,1,0:T(8,128)} %bitcast.14, f32[3,24]{1,0:T(4,128)} %refs_1_.1, f32[3,24]{1,0:T(4,128)} %refs_2_.1, f32[3,24,24]{2,1,0:T(8,128)} %refs_3_.1, f32[3,24,24]{2,1,0:T(8,128)} %refs_4_.1, f32[3,24]{1,0:T(4,128)} %refs_5_.1, ...), custom_call_target="tpu_custom_call" | custom-call | tf_op jit(solution)/shard_map/flow/pallas_call | solution.py:591
  48.2 2.1 %deliver.1 = (f32[8,12,1,32]{3,2,1,0:T(1,128)}, f32[1,64,48]{2,1,0:T(8,128)}, f32[1]{0:T(128)}) custom-call(f32[8,12,32]{2,1,0:T(8,128)} %get-tuple-element.9.mid, f32[1,64,48]{2,1,0:T(8,128)} %get-tuple-element.10.top, f32[1]{0:T(128)} %get-tuple-element.11.lik), custom_call_target="tpu_custom_call" | custom-call | tf_op jit(solution)/shard_map/deliver/pallas_call | solution.py:625
where the time goes:
time: 50.6 us; the launch traced here: 50.4 us
  Pallas kernels  49.6 us (98%)
  between operations  0.81 us (2%)
    pallas_call x1, Pallas kernels, body(): pl.pallas_call(functools.partial(kernel, (n_rows, n_chan, split, height,...  47.5 us
    pallas_call x1, Pallas kernels, body(): pl.pallas_call(deliver, out_shape=(jax.ShapeDtypeStruct((n_imgs, half, ow...  2.06 us

commit v1 on v0

v1 whole, which is shorter than its diff:
```python
import functools
import math

import jax
import jax.numpy as jnp
from jax import lax
from jax.experimental import pallas as pl
from jax.experimental.pallas import tpu as pltpu
from jax.sharding import PartitionSpec as P

MESH = pl.DeviceIdType.MESH
LANES = 128
CHUNK = 1024
FINE = lax.Precision.HIGHEST
log_two_pi = math.log(2.0 * math.pi)
f32 = jnp.float32
bf16 = jnp.bfloat16


def iota(shape, dim):
    return lax.broadcasted_iota(jnp.int32, shape, dim)


def dot_nt(a, b, precision=None):
    return lax.dot_general(
        a, b, (((1,), (1,)), ((), ())), preferred_element_type=f32, precision=precision
    )


def roll(x, amount):
    n = x.shape[1]
    amount = amount % n
    return x if amount == 0 else pltpu.roll(x, amount, 1)


def keep(x, ok):
    return jnp.where(ok, x, 0.0)


def mid_map(channels):
    i = iota((channels, channels), 0)
    j = iota((channels, channels), 1)
    source = jnp.where(i < 12, i, jnp.where(i < 16, i + 8, i - 4))
    return jnp.where(source == j, 1.0, 0.0)


def eye_map(channels):
    return jnp.where(iota((channels, channels), 0) == iota((channels, channels), 1), 1.0, 0.0)


def squeeze_map(channels):
    i = iota((channels, channels), 0)
    j = iota((channels, channels), 1)
    low = 4 * lax.rem(i, 8) + lax.div(i, 8)
    k = i - 32
    place = 2 * lax.div(k, 8) + 1 - lax.div(lax.rem(k + 64, 8), 4)
    high = 4 * (8 + lax.rem(k + 64, 4)) + place
    return jnp.where(jnp.where(i < 32, low, high) == j, 1.0, 0.0)


def split_two(x):
    high = x.astype(bf16).astype(f32)
    return high, x - high


def mixing(lower, upper, diag_row, gain_row, shift_row, out_map, in_map, exact):
    channels = lower.shape[0]
    i = iota((channels, channels), 0)
    j = iota((channels, channels), 1)
    eye = jnp.where(i == j, 1.0, 0.0)
    low = jnp.where(i > j, lower, 0.0) + eye
    upp = (jnp.where(i < j, upper, 0.0) + eye * jnp.exp(diag_row)) * jnp.exp(gain_row)
    rows = jnp.dot(out_map, low, precision=FINE, preferred_element_type=f32)
    mat = jnp.dot(rows, upp, precision=FINE, preferred_element_type=f32)
    bias = jnp.sum(mat * shift_row, axis=1, keepdims=True)
    if in_map is not None:
        mat = dot_nt(mat, in_map, FINE)
    high, rest = split_two(mat)
    parts = [high, rest] if exact else [high, high, rest]
    return jnp.concatenate(parts, axis=1).astype(bf16), bias


def mapped_column(row, mapping):
    return jnp.sum(mapping * row, axis=1, keepdims=True)


def prepare(p, s):
    steps_mid, channels = p["shift_mid"].shape
    steps_top, top_channels = p["shift_top"].shape
    hidden = p["w2_mid"].shape[1]
    half = channels // 2
    mapping = mid_map(channels)
    natural = eye_map(top_channels)
    for k in range(steps_mid):
        mat, bias = mixing(
            p["lower_mid"][k],
            p["upper_mid"][k],
            p["diag_mid"][k : k + 1, :],
            p["gain_mid"][k : k + 1, :],
            p["shift_mid"][k : k + 1, :],
            mapping,
            None if k == 0 else mapping,
            k == 0,
        )
        s["mix_mid"][k, :, : mat.shape[1]] = mat
        s["mix_bias_mid"][k] = jnp.broadcast_to(bias, (channels, LANES))
        s["b3_mid"][k] = jnp.broadcast_to(
            mapped_column(p["third_bias_mid"][k : k + 1, :], mapping), (channels, LANES)
        )
    for k in range(steps_top):
        mat, bias = mixing(
            p["lower_top"][k],
            p["upper_top"][k],
            p["diag_top"][k : k + 1, :],
            p["gain_top"][k : k + 1, :],
            p["shift_top"][k : k + 1, :],
            natural,
            squeeze_map(top_channels) if k == 0 else None,
            False,
        )
        s["mix_top"][k, :, : mat.shape[1]] = mat
        s["mix_bias_top"][k] = jnp.broadcast_to(bias, (top_channels, LANES))
        s["b3_top"][k] = jnp.broadcast_to(
            mapped_column(p["third_bias_top"][k : k + 1, :], natural), (top_channels, LANES)
        )
    for k in range(steps_mid):
        taps = []
        for tap in range(9):
            extra = [jnp.zeros((16 - half, hidden), f32)]
            if tap == 4:
                row = p["first_bias_mid"][k : k + 1, :].astype(f32)
                extra = [row, jnp.zeros((15 - half, hidden), f32)]
            taps.append(jnp.concatenate([p["w1_mid"][k, tap].astype(f32)] + extra, axis=0))
        s["w1t_mid"][k] = jnp.transpose(jnp.concatenate(taps, axis=0)).astype(bf16)
        s["w2t_mid"][k] = jnp.transpose(p["w2_mid"][k].astype(f32)).astype(bf16)
        s["b2_mid"][k] = jnp.transpose(
            jnp.broadcast_to(p["second_bias_mid"][k : k + 1, :], (LANES, hidden))
        )
        for tap in range(9):
            w = p["w3_mid"][k, tap * channels : (tap + 1) * channels, :].astype(f32)
            w = jnp.concatenate([w[:12], w[20:24], w[12:20]], axis=0)
            s["w3f_mid"][tap * channels : (tap + 1) * channels, :] = w
        s["w3p_mid"][k] = s["w3f_mid"][...].astype(bf16)
    for k in range(steps_top):
        row = p["first_bias_top"][k : k + 1, :].astype(f32)
        w = jnp.concatenate(
            [p["w1_top"][k].astype(f32), row, jnp.zeros((7, hidden), f32)], axis=0
        )
        s["w1t_top"][k] = jnp.transpose(w).astype(bf16)
        s["w2t_top"][k] = jnp.transpose(p["w2_top"][k].astype(f32)).astype(bf16)
        s["b2_top"][k] = jnp.transpose(
            jnp.broadcast_to(p["second_bias_top"][k : k + 1, :], (LANES, hidden))
        )


def wide(x, n):
    return jnp.concatenate([x] * (n // LANES), axis=1)


def lane_of(n):
    return lax.rem(iota((1, n), 1), LANES)


def edge_mid(x, dr):
    lane = iota((1, LANES), 1)
    if dr > 0:
        return keep(roll(x, -32), lane < 96)
    return keep(roll(x, 32), lane >= 32)


def edge_top(x, dr):
    lane = iota((1, LANES), 1)
    odd = lax.rem(lane, 2) == 1
    if dr > 0:
        return jnp.where(odd, keep(roll(x, -31), lane < 96), roll(x, -1))
    return jnp.where(odd, roll(x, 1), keep(roll(x, 31), lane >= 32))


def shift_col(x, dc, stride):
    n = x.shape[1]
    col = lax.rem(iota((1, n), 1), 32)
    if dc > 0:
        return keep(roll(x, -stride), col < 32 - stride)
    return keep(roll(x, stride), col >= stride)


def gather(y_ref, tap_rows, lo, hi, n, edge, stride):
    total = None
    for dc in (0, -1, 1):
        base = 4 + dc
        part = y_ref[base * tap_rows : (base + 1) * tap_rows, lo:hi]
        for dr in (-1, 1):
            tap = base + 3 * dr
            rows = slice(tap * tap_rows, (tap + 1) * tap_rows)
            if dr > 0 and hi == n:
                moved = [edge(y_ref[rows, :LANES], dr)]
                if hi - lo > LANES:
                    moved = [y_ref[rows, lo + LANES : hi]] + moved
                moved = jnp.concatenate(moved, axis=1) if len(moved) > 1 else moved[0]
            elif dr < 0 and lo == 0:
                moved = [edge(y_ref[rows, n - LANES : n], dr)]
                if hi - lo > LANES:
                    moved = moved + [y_ref[rows, : hi - LANES]]
                moved = jnp.concatenate(moved, axis=1) if len(moved) > 1 else moved[0]
            else:
                moved = y_ref[rows, lo + dr * LANES : hi + dr * LANES]
            part = part + moved
        if dc != 0:
            part = shift_col(part, dc, stride)
        total = part if total is None else total + part
    return total


def gated(g):
    e = jnp.exp(-jnp.abs(g))
    inv = 1.0 / (1.0 + e)
    gate = jnp.where(g >= 0, inv, e * inv)
    return gate, jnp.minimum(g, 0.0) - jnp.log(1.0 + e)


def fold(x):
    total = x[:, :LANES]
    for at in range(LANES, x.shape[1], LANES):
        total = total + x[:, at : at + LANES]
    return total


def mix(mat, bias, x, exact):
    n = x.shape[1]
    if exact:
        stack = [x, x]
    else:
        high, rest = split_two(x)
        stack = [high, rest, high]
    stack = jnp.concatenate(stack, axis=0).astype(bf16)
    return jnp.dot(mat, stack, preferred_element_type=f32) + wide(bias, n)


def product(first, second, third, bias, spread, y_ref, rows, lo):
    n = spread.shape[1]
    h = jnp.dot(first[...], spread, preferred_element_type=f32)
    h = jnp.maximum(h, 0.0).astype(bf16)
    h = jnp.dot(second[...], h, preferred_element_type=f32)
    h = jnp.maximum(h + wide(bias[...], n), 0.0).astype(bf16)
    y_ref[:rows, lo : lo + n] = jnp.dot(third[...], h, preferred_element_type=f32)


def mid_step(s, k, exact):
    state, u_ref, q_ref, y_ref = s["state"], s["u"], s["q"], s["y"]
    channels, n = state.shape
    block = 4 * LANES
    sub = iota((8, 1), 0)
    mat = s["mix_mid"][k, :, : (2 if exact else 3) * channels]
    for lo in range(0, n, block):
        u_ref[:, lo : lo + block] = mix(
            mat, s["mix_bias_mid"][k], state[:, lo : lo + block], exact
        )
    for lo in range(0, n, block):
        q = u_ref[:16, lo : lo + block]
        q = jnp.concatenate([q[:8], jnp.where(sub == 4, 1.0, q[8:])], axis=0)
        for dc in (-1, 0, 1):
            x = q if dc == 0 else shift_col(q, dc, 1)
            q_ref[dc + 1, :, LANES + lo : LANES + lo + block] = x.astype(bf16)
            if lo == 0:
                q_ref[dc + 1, :, LANES + n :] = edge_mid(x[:, :LANES], 1).astype(bf16)
            if lo + block == n:
                q_ref[dc + 1, :, :LANES] = edge_mid(x[:, block - LANES :], -1).astype(bf16)
    for lo in range(0, n, min(CHUNK, n)):
        taps = []
        for dr in (-1, 0, 1):
            at = lo + LANES * (1 + dr)
            for dc in (-1, 0, 1):
                taps.append(q_ref[dc + 1, :, at : at + min(CHUNK, n)])
        product(
            s["w1t_mid"].at[k],
            s["w2t_mid"].at[k],
            s["w3p_mid"].at[k],
            s["b2_mid"].at[k],
            jnp.concatenate(taps, axis=0),
            y_ref,
            9 * channels,
            lo,
        )
    score = None
    width = 2 * LANES
    for lo in range(0, n, width):
        out = gather(y_ref, channels, lo, lo + width, n, edge_mid, 1) + wide(s["b3_mid"][k], width)
        gate, logs = gated(out[:16] + 2.0)
        logs = fold(logs)
        score = logs if score is None else score + logs
        u = u_ref[:, lo : lo + width]
        state[:8, lo : lo + width] = u[:8]
        late = (u[8:16] + out[8:16]) * pltpu.roll(gate[8:16], 4, 0)
        state[8:16, lo : lo + width] = jnp.where(sub < 4, u[8:16], late)
        state[16:, lo : lo + width] = (u[16:] + out[16:]) * gate[:8]
    return keep(score, iota((16, 1), 0) < channels // 2)


def squeeze(s):
    state, top = s["state"], s["top"]
    odd = lax.rem(iota((1, LANES), 1), 2) == 1
    sub = iota((8, 1), 0)
    for v in range(4):
        tails = []
        for i in range(2):
            t = (2 * v + i) * LANES
            a = state[8:, t : t + LANES]
            t = t + 8 * LANES
            b = state[8:, t : t + LANES]
            even_col = jnp.where(odd, roll(b, 1), a)
            odd_col = jnp.where(odd, b, roll(a, -1))
            cols = slice(v * LANES, (v + 1) * LANES)
            top[16 * i : 16 * i + 8, cols] = even_col[8:]
            top[16 * i + 8 : 16 * i + 16, cols] = odd_col[8:]
            top[32 + 8 * i : 40 + 8 * i, cols] = jnp.where(
                sub < 4, pltpu.roll(odd_col[:8], 4, 0), even_col[:8]
            )


def top_step(s, k):
    state, u_ref, q_ref, y_ref = s["top"], s["u_top"], s["q_top"], s["y_top"]
    channels, n = state.shape
    half = channels // 2
    mat = s["mix_top"][k, :, : 3 * channels]
    u_ref[...] = mix(mat, s["mix_bias_top"][k], state[...], False)
    q = u_ref[:half, :]
    for dc in (-1, 0, 1):
        x = q if dc == 0 else shift_col(q, dc, 2)
        q_ref[dc + 1, :, LANES : LANES + n] = x
        q_ref[dc + 1, :, LANES + n :] = edge_top(x[:, :LANES], 1)
        q_ref[dc + 1, :, :LANES] = edge_top(x[:, n - LANES :], -1)
    ones = jnp.where(iota((8, min(CHUNK, n)), 0) == 0, 1.0, 0.0)
    for lo in range(0, n, min(CHUNK, n)):
        taps = []
        for dr in (-1, 0, 1):
            at = lo + LANES * (1 + dr)
            for dc in (-1, 0, 1):
                taps.append(q_ref[dc + 1, :, at : at + min(CHUNK, n)])
        product(
            s["w1t_top"].at[k],
            s["w2t_top"].at[k],
            s["w3_top"].at[k],
            s["b2_top"].at[k],
            jnp.concatenate(taps + [ones], axis=0).astype(bf16),
            y_ref,
            9 * channels,
            lo,
        )
    score = None
    width = LANES
    for lo in range(0, n, width):
        out = gather(y_ref, channels, lo, lo + width, n, edge_top, 2) + wide(s["b3_top"][k], width)
        gate, logs = gated(out[:half] + 2.0)
        score = logs if score is None else score + logs
        state[:half, lo : lo + width] = u_ref[:half, lo : lo + width]
        state[half:, lo : lo + width] = (u_ref[half:, lo : lo + width] + out[half:]) * gate
    return score


def work_scratch(steps_mid, steps_top, hidden, channels, top_channels, cells):
    n_top = cells // 4
    return {
        "mix_mid": pltpu.VMEM((steps_mid, channels, 3 * channels), bf16),
        "mix_bias_mid": pltpu.VMEM((steps_mid, channels, LANES), f32),
        "b3_mid": pltpu.VMEM((steps_mid, channels, LANES), f32),
        "mix_top": pltpu.VMEM((steps_top, top_channels, 3 * top_channels), bf16),
        "mix_bias_top": pltpu.VMEM((steps_top, top_channels, LANES), f32),
        "b3_top": pltpu.VMEM((steps_top, top_channels, LANES), f32),
        "w1t_mid": pltpu.VMEM((steps_mid, hidden, 144), bf16),
        "w2t_mid": pltpu.VMEM((steps_mid, hidden, hidden), bf16),
        "b2_mid": pltpu.VMEM((steps_mid, hidden, LANES), f32),
        "w3f_mid": pltpu.VMEM((9 * channels, hidden), f32),
        "w3p_mid": pltpu.VMEM((steps_mid, 9 * channels, hidden), bf16),
        "w1t_top": pltpu.VMEM((steps_top, hidden, 9 * top_channels // 2 + 8), bf16),
        "w2t_top": pltpu.VMEM((steps_top, hidden, hidden), bf16),
        "b2_top": pltpu.VMEM((steps_top, hidden, LANES), f32),
        "state": pltpu.VMEM((channels, cells), f32),
        "u": pltpu.VMEM((channels, cells), f32),
        "q": pltpu.VMEM((3, 16, cells + 2 * LANES), bf16),
        "y": pltpu.VMEM((9 * channels, cells), f32),
        "top": pltpu.VMEM((top_channels, n_top), f32),
        "u_top": pltpu.VMEM((top_channels, n_top), f32),
        "q_top": pltpu.VMEM((3, top_channels // 2, n_top + 2 * LANES), f32),
        "y_top": pltpu.VMEM((9 * top_channels, n_top), f32),
        "turned": pltpu.VMEM((n_top, LANES), f32),
    }


NAMES = (
    "shift_mid",
    "gain_mid",
    "lower_mid",
    "upper_mid",
    "diag_mid",
    "w1_mid",
    "first_bias_mid",
    "w2_mid",
    "second_bias_mid",
    "w3_mid",
    "third_bias_mid",
    "shift_top",
    "gain_top",
    "lower_top",
    "upper_top",
    "diag_top",
    "w1_top",
    "first_bias_top",
    "w2_top",
    "second_bias_top",
    "w3_top",
    "third_bias_top",
)


def parameters(params):
    (
        shift_mid, gain_mid, lower_mid, upper_mid, diag_mid, first_mid, first_bias_mid, second_mid,
        second_bias_mid, third_mid, third_bias_mid, shift_top, gain_top, lower_top, upper_top,
        diag_top, first_top, first_bias_top, second_top, second_bias_top, third_top, third_bias_top,
    ) = params
    steps_mid, hidden = first_bias_mid.shape
    steps_top = first_bias_top.shape[0]
    w1_top = first_top.reshape(steps_top, -1, hidden)
    w3_mid = third_mid.transpose(0, 1, 3, 2).reshape(steps_mid, -1, hidden)
    w3_top = third_top.transpose(0, 1, 3, 2).reshape(steps_top, -1, hidden)
    return (
        shift_mid, gain_mid, lower_mid, upper_mid, diag_mid, first_mid, first_bias_mid, second_mid,
        second_bias_mid, w3_mid, third_bias_mid, shift_top, gain_top, lower_top, upper_top,
        diag_top, w1_top, first_bias_top, second_top, second_bias_top, w3_top, third_bias_top,
    )


def kernel(dims, keys, *refs):
    n_rows, n_chan, height, width, count = dims
    sources, refs = refs[:count], refs[count:]
    (mid_out, top_out, lik_out), refs = refs[:3], refs[3:]
    held, refs = refs[:count], refs[count:]
    s, refs = dict(zip(keys, refs)), refs[len(keys) :]
    outbox, inbox, z_send, z_recv, w_sem, send_sem, recv_sem, z_send_sem, z_recv_sem = refs
    images = held[0]
    p = dict(zip(NAMES, held[1:]))
    s["w3_top"] = p["w3_top"]
    peers = n_rows * n_chan
    b = lax.axis_index("batch")
    r = lax.axis_index("rows")
    c = lax.axis_index("chan")
    me = r * n_chan + c
    quad = lax.div(r, 2)
    side = lax.rem(r, 2)

    def device(row, chan):
        return {"batch": b, "rows": row, "chan": chan}

    def swap(y):
        return y + lax.div(y, 2) * (5 - 2 * y)

    def place(q):
        at = lax.rem(q, n_chan)
        return lax.div(q, n_chan), 2 * swap(lax.div(at, 2)) + 1 - lax.rem(at, 2)

    rank = r * n_chan + 2 * swap(lax.div(c, 2)) + 1 - lax.rem(c, 2)

    first = pltpu.make_async_copy(sources[0], held[0], w_sem.at[0])
    first.start()
    barrier = pltpu.get_barrier_semaphore()

    def greet(q, carry):
        row, chan = place(q)
        pl.semaphore_signal(barrier, inc=1, device_id=device(row, chan), device_id_type=MESH)
        return carry

    lax.fori_loop(rank + 1, peers, greet, 0)
    first.wait()
    for dest in range(n_chan):
        x = images[dest]
        x = jnp.concatenate([x[:8], x[8:16], x[16:], jnp.zeros((8, width), f32)], axis=1)
        outbox[dest] = pltpu.roll(x, quad * 32, 1).astype(bf16)
    @pl.when(rank > 0)
    def _():
        pl.semaphore_wait(barrier, rank)

    def send(q, carry):
        row, chan = place(q)
        pltpu.make_async_remote_copy(
            src_ref=outbox.at[chan],
            dst_ref=inbox.at[me],
            send_sem=send_sem,
            recv_sem=recv_sem.at[me],
            device_id=device(row, chan),
            device_id_type=MESH,
        ).start()
        return carry

    def arrive(q, carry):
        row, chan = place(q)
        slot = row * n_chan + chan
        pltpu.make_async_remote_copy(
            src_ref=outbox.at[0],
            dst_ref=inbox.at[slot],
            send_sem=send_sem,
            recv_sem=recv_sem.at[slot],
            device_id=device(r, c),
            device_id_type=MESH,
        ).wait_recv()
        return carry

    lax.fori_loop(0, rank, send, 0)
    copies = []
    for at in range(1, count):
        copy = pltpu.make_async_copy(sources[at], held[at], w_sem.at[at])
        copy.start()
        copies.append(copy)
    inbox[me] = outbox[c]
    for copy in copies:
        copy.wait()
    prepare(p, s)
    channels = p["shift_mid"].shape[1]
    top_channels = p["shift_top"].shape[1]
    half = channels // 2
    cells = height * width
    fixed = cells * (jnp.sum(p["gain_mid"][...]) + jnp.sum(p["diag_mid"][...]))
    fixed = fixed + cells // 4 * (jnp.sum(p["gain_top"][...]) + jnp.sum(p["diag_top"][...]))
    fixed = fixed - 0.5 * log_two_pi * channels * cells

    lax.fori_loop(rank + 1, peers, lambda q, x: send(q, arrive(q, x)), 0)
    lax.fori_loop(0, rank, arrive, 0)

    state = s["state"]
    lane = iota((1, LANES), 1)
    for t in range(height // 4):
        letters = [inbox[16 * k + t].astype(f32) for k in range(4)]
        for slab in range(3):
            x = letters[(3 - slab) % 4]
            for k in range(3):
                x = jnp.where(lax.div(lane, 32) == k, letters[(k - slab) % 4], x)
            state[8 * slab : 8 * slab + 8, t * LANES : (t + 1) * LANES] = roll(x, -32 * slab)

    score = None
    for k in range(p["shift_mid"].shape[0]):
        logs = mid_step(s, k, k == 0)
        score = logs if score is None else score + logs

    for to in range(n_chan):
        start = pl.multiple_of((side * n_chan + to) * LANES, LANES)
        z = state[:16, pl.ds(start, LANES)]
        z_send[to] = jnp.where(
            lane < 32,
            pltpu.roll(z[:8], LANES - quad * 32, 1),
            pltpu.roll(z[8:], LANES + 32 - quad * 32, 1),
        )
    z_copies = []
    for d in range(1, n_chan):
        other = lax.rem(c + d, n_chan)
        copy = pltpu.make_async_remote_copy(
            src_ref=z_send.at[other],
            dst_ref=z_recv.at[c],
            send_sem=z_send_sem.at[d],
            recv_sem=z_recv_sem.at[d],
            device_id=device(r, other),
            device_id_type=MESH,
        )
        copy.start()
        z_copies.append(copy)
    z_recv[c] = z_send[c]

    squares = fold(state[:16, :] * state[:16, :])
    score = score - 0.5 * keep(squares, iota((16, 1), 0) < half)
    squeeze(s)
    score_top = None
    for k in range(p["shift_top"].shape[0]):
        logs = top_step(s, k)
        score_top = logs if score_top is None else score_top + logs
    top = s["top"]
    squares = fold(top[...] * top[...])
    total = jnp.sum(score, axis=0, keepdims=True) + jnp.sum(score_top, axis=0, keepdims=True)
    total = total - 0.5 * jnp.sum(squares, axis=0, keepdims=True)
    lik_out[0] = (jnp.sum(total) + fixed) / (channels * cells)
    turned = s["turned"]
    for v in range(4):
        turned[v * LANES : (v + 1) * LANES, :top_channels] = jnp.transpose(
            top[:, v * LANES : (v + 1) * LANES]
        )
    for v in range(4):
        start = v * LANES + quad * 32 + side
        top_out[0, v * 16 : (v + 1) * 16, :] = turned[pl.ds(start, 16, stride=2), :][
            :, :top_channels
        ]

    for d in range(1, n_chan):
        pltpu.make_async_remote_copy(
            src_ref=z_send.at[0],
            dst_ref=z_recv.at[lax.rem(c + n_chan - d, n_chan)],
            send_sem=z_send_sem.at[d],
            recv_sem=z_recv_sem.at[d],
            device_id=device(r, c),
            device_id_type=MESH,
        ).wait_recv()
    for img in range(n_chan):
        z = z_recv[img]
        mid_out[img, :8, :] = z[:, :width]
        mid_out[img, 8:, :] = z[:4, width : 2 * width]
    for copy in z_copies:
        copy.wait_send()
    pltpu.make_async_remote_copy(
        src_ref=inbox.at[pl.ds(0, peers - 1)],
        dst_ref=inbox.at[pl.ds(0, peers - 1)],
        send_sem=send_sem,
        recv_sem=recv_sem.at[0],
        device_id=device(r, c),
        device_id_type=MESH,
    ).wait_send()


def deliver(mid, top, lik, mid_out, top_out, lik_out):
    for img in range(mid.shape[0]):
        mid_out[img, :, 0, :] = mid[img]
    top_out[...] = top[...]
    lik_out[0] = lik[0]


def body(sizes, images, *params):
    n_rows, n_chan = sizes
    n_imgs, channels, own_rows, width = images.shape
    peers = n_rows * n_chan
    height = own_rows * peers
    params = parameters(params)
    hidden = params[6].shape[1]
    steps_mid, steps_top = params[0].shape[0], params[11].shape[0]
    top_channels = params[11].shape[1]
    half = channels // 2
    cells = height * width
    own = cells // 4 // n_rows
    operands = (images.reshape(n_imgs, channels, width),) + params
    vmem = pl.BlockSpec(memory_space=pltpu.VMEM)
    smem = pl.BlockSpec(memory_space=pltpu.SMEM)
    count = len(operands)
    work = work_scratch(steps_mid, steps_top, hidden, channels, top_channels, cells)
    mid, top, lik = pl.pallas_call(
        functools.partial(kernel, (n_rows, n_chan, height, width, count), list(work)),
        out_shape=(
            jax.ShapeDtypeStruct((n_imgs, half, width), f32),
            jax.ShapeDtypeStruct((1, own, top_channels), f32),
            jax.ShapeDtypeStruct((1,), f32),
        ),
        in_specs=[pl.BlockSpec(memory_space=pl.ANY)] * count,
        out_specs=(vmem, vmem, smem),
        scratch_shapes=[pltpu.VMEM(x.shape, x.dtype) for x in operands]
        + list(work.values())
        + [
            pltpu.VMEM((n_chan, 8, LANES), bf16),
            pltpu.VMEM((peers, 8, LANES), bf16),
            pltpu.VMEM((n_chan, 8, LANES), f32),
            pltpu.VMEM((n_chan, 8, LANES), f32),
            pltpu.SemaphoreType.DMA((count,)),
            pltpu.SemaphoreType.DMA,
            pltpu.SemaphoreType.DMA((peers,)),
            pltpu.SemaphoreType.DMA((n_chan,)),
            pltpu.SemaphoreType.DMA((n_chan,)),
        ],
        compiler_params=pltpu.CompilerParams(
            collective_id=0, has_side_effects=True, vmem_limit_bytes=56 * 1024 * 1024
        ),
        name="flow",
    )(*operands)
    latent_mid, top, lik = pl.pallas_call(
        deliver,
        out_shape=(
            jax.ShapeDtypeStruct((n_imgs, half, own_rows, width), f32),
            jax.ShapeDtypeStruct(top.shape, f32),
            jax.ShapeDtypeStruct(lik.shape, f32),
        ),
        in_specs=[vmem, vmem, smem],
        out_specs=(vmem, vmem, smem),
        name="deliver",
    )(mid, top, lik)
    latent_top = top.reshape(1, -1, width // 2, top_channels).transpose(0, 3, 1, 2)
    return latent_mid, latent_top, lik


def solution(mesh):
    sizes = (mesh.shape["rows"], mesh.shape["chan"])
    placed = (P("batch", None, ("rows", "chan"), None),) + (P(),) * 22
    return jax.shard_map(
        functools.partial(body, sizes),
        mesh=mesh,
        in_specs=placed,
        out_specs=(
            P("batch", None, ("rows", "chan"), None),
            P(("batch", "chan"), None, "rows", None),
            P(("batch", "chan")),
        ),
        check_vma=False,
    )
```

time: 50.6 us -> 39.2 us (0.77)
  Pallas kernels: 49.6 us -> 38.3 us
    pallas_call x1, Pallas kernels: 47.5 us -> 36.3 us  [body(): pl.pallas_call(functools.partial(kernel, (n_rows, n_chan, height, width,...]
where the time goes in v1:
time: 39.2 us; the launch traced here: 39 us
  Pallas kernels  38.3 us (98%)
  between operations  0.65 us (2%)
    pallas_call x1, Pallas kernels, body(): pl.pallas_call(functools.partial(kernel, (n_rows, n_chan, height, width,...  36.3 us
    pallas_call x1, Pallas kernels, body(): pl.pallas_call(deliver, out_shape=(jax.ShapeDtypeStruct((n_imgs, half, ow...  2.06 us

profile of v1, /device:TPU:1, one launch (start us, length us, event | category | flops | bytes accessed | tf_op | source)
XLA Modules:
  0.0 39.0 jit_solution(1431010198143644659)
XLA Ops:
  0.6 36.3 %flow.1 = (f32[8,12,32]{2,1,0:T(8,128)}, f32[1,64,48]{2,1,0:T(8,128)}, f32[1]{0:T(128)}) custom-call(f32[8,24,32]{2,1,0:T(8,128)} %bitcast.14, f32[3,24]{1,0:T(4,128)} %refs_1_.1, f32[3,24]{1,0:T(4,128)} %refs_2_.1, f32[3,24,24]{2,1,0:T(8,128)} %refs_3_.1, f32[3,24,24]{2,1,0:T(8,128)} %refs_4_.1, f32[3,24]{1,0:T(4,128)} %refs_5_.1, ...), custom_call_target="tpu_custom_call" | custom-call | tf_op jit(solution)/shard_map/flow/pallas_call | solution.py:638
  36.9 2.1 %deliver.1 = (f32[8,12,1,32]{3,2,1,0:T(1,128)}, f32[1,64,48]{2,1,0:T(8,128)}, f32[1]{0:T(128)}) custom-call(f32[8,12,32]{2,1,0:T(8,128)} %get-tuple-element.9.mid, f32[1,64,48]{2,1,0:T(8,128)} %get-tuple-element.10.top, f32[1]{0:T(128)} %get-tuple-element.11.lik), custom_call_target="tpu_custom_call" | custom-call | tf_op jit(solution)/shard_map/deliver/pallas_call | solution.py:665

commit v2 on v1

--- a/solution.py
+++ b/solution.py
@@ -451,36 +451,38 @@
     def device(row, chan):
         return {"batch": b, "rows": row, "chan": chan}
 
-    def swap(y):
-        return y + lax.div(y, 2) * (5 - 2 * y)
-
-    def place(q):
-        at = lax.rem(q, n_chan)
-        return lax.div(q, n_chan), 2 * swap(lax.div(at, 2)) + 1 - lax.rem(at, 2)
-
-    rank = r * n_chan + 2 * swap(lax.div(c, 2)) + 1 - lax.rem(c, 2)
+    def key(row, chan):
+        y = chan // 2
+        far = row // 4
+        when = 15 * row * (1 - far) + (53 + 4 * row) * far + 12 * (y + y // 2 * (5 - 2 * y))
+        return ((when + 3 * (1 - chan % 2)) * n_rows + row) * n_chan + chan
+
+    order = sorted((key(row, chan), row, chan) for row in range(n_rows) for chan in range(n_chan))
+    mine = key(r, c)
 
     first = pltpu.make_async_copy(sources[0], held[0], w_sem.at[0])
     first.start()
     barrier = pltpu.get_barrier_semaphore()
 
-    def greet(q, carry):
-        row, chan = place(q)
-        pl.semaphore_signal(barrier, inc=1, device_id=device(row, chan), device_id_type=MESH)
-        return carry
-
-    lax.fori_loop(rank + 1, peers, greet, 0)
+    for at, row, chan in order[1:]:
+
+        @pl.when(at > mine)
+        def _():
+            pl.semaphore_signal(barrier, inc=1, device_id=device(row, chan), device_id_type=MESH)
+
+    earlier = 0
+    for at, _, _ in order:
+        earlier = earlier + jnp.where(at < mine, 1, 0)
     first.wait()
     for dest in range(n_chan):
         x = images[dest]
         x = jnp.concatenate([x[:8], x[8:16], x[16:], jnp.zeros((8, width), f32)], axis=1)
         outbox[dest] = pltpu.roll(x, quad * 32, 1).astype(bf16)
-    @pl.when(rank > 0)
+    @pl.when(earlier > 0)
     def _():
-        pl.semaphore_wait(barrier, rank)
-
-    def send(q, carry):
-        row, chan = place(q)
+        pl.semaphore_wait(barrier, earlier)
+
+    def send(row, chan):
         pltpu.make_async_remote_copy(
             src_ref=outbox.at[chan],
             dst_ref=inbox.at[me],
@@ -489,10 +491,8 @@
             device_id=device(row, chan),
             device_id_type=MESH,
         ).start()
-        return carry
-
-    def arrive(q, carry):
-        row, chan = place(q)
+
+    def arrive(row, chan):
         slot = row * n_chan + chan
         pltpu.make_async_remote_copy(
             src_ref=outbox.at[0],
@@ -502,9 +502,13 @@
             device_id=device(r, c),
             device_id_type=MESH,
         ).wait_recv()
-        return carry
-
-    lax.fori_loop(0, rank, send, 0)
+
+    for at, row, chan in order[:-1]:
+
+        @pl.when(at < mine)
+        def _():
+            send(row, chan)
+
     copies = []
     for at in range(1, count):
         copy = pltpu.make_async_copy(sources[at], held[at], w_sem.at[at])
@@ -522,8 +526,19 @@
     fixed = fixed + cells // 4 * (jnp.sum(p["gain_top"][...]) + jnp.sum(p["diag_top"][...]))
     fixed = fixed - 0.5 * log_two_pi * channels * cells
 
-    lax.fori_loop(rank + 1, peers, lambda q, x: send(q, arrive(q, x)), 0)
-    lax.fori_loop(0, rank, arrive, 0)
+    for at, row, chan in order[1:]:
+
+        @pl.when(at > mine)
+        def _():
+            arrive(row, chan)
+            send(row, chan)
+
+    for at, row, chan in order[:-1]:
+
+        @pl.when(at < mine)
+        def _():
+            arrive(row, chan)
+
 
     state = s["state"]
     lane = iota((1, LANES), 1)
@@ -638,8 +653,8 @@
     mid, top, lik = pl.pallas_call(
         functools.partial(kernel, (n_rows, n_chan, height, width, count), list(work)),
         out_shape=(
-            jax.ShapeDtypeStruct((n_imgs, half, width), f32),
-            jax.ShapeDtypeStruct((1, own, top_channels), f32),
+            pltpu.VMEM((n_imgs, half, width), f32),
+            pltpu.VMEM((1, own, top_channels), f32),
             jax.ShapeDtypeStruct((1,), f32),
         ),
         in_specs=[pl.BlockSpec(memory_space=pl.ANY)] * count,
@@ -671,6 +686,7 @@
         ),
         in_specs=[vmem, vmem, smem],
         out_specs=(vmem, vmem, smem),
+        compiler_params=pltpu.CompilerParams(vmem_limit_bytes=4 * 1024 * 1024),
         name="deliver",
     )(mid, top, lik)
     latent_top = top.reshape(1, -1, width // 2, top_channels).transpose(0, 3, 1, 2)

time: 39.2 us -> 39.5 us (level)
  the two profiles are of different devices: /device:TPU:1 before, /device:TPU:205 now
where the time goes in v2:
time: 39.5 us; the launch traced here: 39.3 us
  Pallas kernels  38.6 us (98%)
  between operations  0.65 us (2%)
    pallas_call x1, Pallas kernels, body(): pl.pallas_call(functools.partial(kernel, (n_rows, n_chan, height, width,...  37.3 us
    pallas_call x1, Pallas kernels, body(): pl.pallas_call(deliver, out_shape=(jax.ShapeDtypeStruct((n_imgs, half, ow...  1.3 us

profile of v2, /device:TPU:205, one launch (start us, length us, event | category | flops | bytes accessed | tf_op | source)
XLA Modules:
  0.0 39.3 jit_solution(6683478340404433479)
XLA Ops:
  0.6 37.3 %flow.1 = (f32[8,12,32]{2,1,0:T(8,128)S(1)}, f32[1,64,48]{2,1,0:T(8,128)S(1)}, f32[1]{0:T(128)}) custom-call(f32[8,24,32]{2,1,0:T(8,128)} %bitcast.14, f32[3,24]{1,0:T(4,128)} %refs_1_.1, f32[3,24]{1,0:T(4,128)} %refs_2_.1, f32[3,24,24]{2,1,0:T(8,128)} %refs_3_.1, f32[3,24,24]{2,1,0:T(8,128)} %refs_4_.1, f32[3,24]{1,0:T(4,128)} %refs_5_.1, ...), custom_call_target="tpu_custom_call" | custom-call | tf_op jit(solution)/shard_map/flow/pallas_call | solution.py:653
  38.0 1.3 %deliver.1 = (f32[8,12,1,32]{3,2,1,0:T(1,128)}, f32[1,64,48]{2,1,0:T(8,128)}, f32[1]{0:T(128)}) custom-call(f32[8,12,32]{2,1,0:T(8,128)S(1)} %get-tuple-element.9.mid, f32[1,64,48]{2,1,0:T(8,128)S(1)} %get-tuple-element.10.top, f32[1]{0:T(128)} %get-tuple-element.11.lik), custom_call_target="tpu_custom_call" | custom-call | tf_op jit(solution)/shard_map/deliver/pallas_call | solution.py:680

commit v3 on v2

--- a/solution.py
+++ b/solution.py
@@ -436,85 +436,104 @@
     (mid_out, top_out, lik_out), refs = refs[:3], refs[3:]
     held, refs = refs[:count], refs[count:]
     s, refs = dict(zip(keys, refs)), refs[len(keys) :]
-    outbox, inbox, z_send, z_recv, w_sem, send_sem, recv_sem, z_send_sem, z_recv_sem = refs
+    outbox, stage, inbox, z_send, z_recv, w_sem, refs = *refs[:6], refs[6:]
+    stage_send, piece_send, stage_sem, hello_sem, piece_sem, z_send_sem, z_recv_sem = refs
     images = held[0]
     p = dict(zip(NAMES, held[1:]))
     s["w3_top"] = p["w3_top"]
-    peers = n_rows * n_chan
     b = lax.axis_index("batch")
     r = lax.axis_index("rows")
     c = lax.axis_index("chan")
-    me = r * n_chan + c
     quad = lax.div(r, 2)
     side = lax.rem(r, 2)
 
     def device(row, chan):
         return {"batch": b, "rows": row, "chan": chan}
 
-    def key(row, chan):
-        y = chan // 2
-        far = row // 4
-        when = 15 * row * (1 - far) + (53 + 4 * row) * far + 12 * (y + y // 2 * (5 - 2 * y))
-        return ((when + 3 * (1 - chan % 2)) * n_rows + row) * n_chan + chan
-
-    order = sorted((key(row, chan), row, chan) for row in range(n_rows) for chan in range(n_chan))
-    mine = key(r, c)
+    chans = []
+    for q in range(n_chan):
+        y = q // 2
+        chans.append(2 * (y + y // 2 * (5 - 2 * y)) + 1 - q % 2)
+    y = lax.div(c, 2)
+    spot = 2 * (y + lax.div(y, 2) * (5 - 2 * y)) + 1 - lax.rem(c, 2)
 
     first = pltpu.make_async_copy(sources[0], held[0], w_sem.at[0])
     first.start()
     barrier = pltpu.get_barrier_semaphore()
-
-    for at, row, chan in order[1:]:
-
-        @pl.when(at > mine)
+    for row in range(1, n_rows):
+
+        @pl.when(row > r)
         def _():
-            pl.semaphore_signal(barrier, inc=1, device_id=device(row, chan), device_id_type=MESH)
-
-    earlier = 0
-    for at, _, _ in order:
-        earlier = earlier + jnp.where(at < mine, 1, 0)
+            pl.semaphore_signal(barrier, inc=1, device_id=device(row, c), device_id_type=MESH)
+
+    for q in range(1, n_chan):
+
+        @pl.when(q > spot)
+        def _():
+            pl.semaphore_signal(
+                barrier, inc=1, device_id=device(r, chans[q]), device_id_type=MESH
+            )
+
     first.wait()
     for dest in range(n_chan):
         x = images[dest]
         x = jnp.concatenate([x[:8], x[8:16], x[16:], jnp.zeros((8, width), f32)], axis=1)
         outbox[dest] = pltpu.roll(x, quad * 32, 1).astype(bf16)
-    @pl.when(earlier > 0)
+
+    @pl.when(r + spot > 0)
     def _():
-        pl.semaphore_wait(barrier, earlier)
-
-    def send(row, chan):
+        pl.semaphore_wait(barrier, r + spot)
+
+    def send_row(row):
         pltpu.make_async_remote_copy(
-            src_ref=outbox.at[chan],
-            dst_ref=inbox.at[me],
-            send_sem=send_sem,
-            recv_sem=recv_sem.at[me],
-            device_id=device(row, chan),
+            src_ref=outbox,
+            dst_ref=stage.at[r],
+            send_sem=stage_send,
+            recv_sem=stage_sem.at[r],
+            device_id=device(row, c),
             device_id_type=MESH,
         ).start()
 
-    def arrive(row, chan):
-        slot = row * n_chan + chan
+    def send_hello(q):
         pltpu.make_async_remote_copy(
-            src_ref=outbox.at[0],
-            dst_ref=inbox.at[slot],
-            send_sem=send_sem,
-            recv_sem=recv_sem.at[slot],
+            src_ref=outbox.at[chans[q]],
+            dst_ref=inbox.at[c, r],
+            send_sem=piece_send,
+            recv_sem=hello_sem.at[c],
+            device_id=device(r, chans[q]),
+            device_id_type=MESH,
+        ).start()
+
+    def send_piece(row, q):
+        pltpu.make_async_remote_copy(
+            src_ref=stage.at[row, chans[q]],
+            dst_ref=inbox.at[c, row],
+            send_sem=piece_send,
+            recv_sem=piece_sem.at[c],
+            device_id=device(r, chans[q]),
+            device_id_type=MESH,
+        ).start()
+
+    def await_copy(ref, sem):
+        pltpu.make_async_remote_copy(
+            src_ref=ref,
+            dst_ref=ref,
+            send_sem=stage_send,
+            recv_sem=sem,
             device_id=device(r, c),
             device_id_type=MESH,
         ).wait_recv()
 
-    for at, row, chan in order[:-1]:
-
-        @pl.when(at < mine)
-        def _():
-            send(row, chan)
-
+    for row in range(n_rows - 1):
+        pl.when(row < r)(functools.partial(send_row, row))
+    for q in range(n_chan - 1):
+        pl.when(q < spot)(functools.partial(send_hello, q))
     copies = []
     for at in range(1, count):
         copy = pltpu.make_async_copy(sources[at], held[at], w_sem.at[at])
         copy.start()
         copies.append(copy)
-    inbox[me] = outbox[c]
+    stage[r] = outbox[...]
     for copy in copies:
         copy.wait()
     prepare(p, s)
@@ -526,24 +545,38 @@
     fixed = fixed + cells // 4 * (jnp.sum(p["gain_top"][...]) + jnp.sum(p["diag_top"][...]))
     fixed = fixed - 0.5 * log_two_pi * channels * cells
 
-    for at, row, chan in order[1:]:
-
-        @pl.when(at > mine)
+    for q in range(1, n_chan):
+
+        @pl.when(q > spot)
         def _():
-            arrive(row, chan)
-            send(row, chan)
-
-    for at, row, chan in order[:-1]:
-
-        @pl.when(at < mine)
+            await_copy(inbox.at[chans[q], 0], hello_sem.at[chans[q]])
+            send_hello(q)
+
+    for row in range(n_rows):
+
+        @pl.when(row != r)
         def _():
-            arrive(row, chan)
-
+            await_copy(stage.at[row], stage_sem.at[row])
+            pl.when(row > r)(functools.partial(send_row, row))
+            for q in range(n_chan):
+                pl.when(q != spot)(functools.partial(send_piece, row, q))
+
+    for row in range(n_rows):
+        inbox[c, row] = stage[row, c]
+    for q in range(n_chan):
+
+        @pl.when(q < spot)
+        def _():
+            await_copy(inbox.at[chans[q], 0], hello_sem.at[chans[q]])
+
+        @pl.when(q != spot)
+        def _():
+            await_copy(inbox.at[chans[q], pl.ds(0, n_rows - 1)], piece_sem.at[chans[q]])
 
     state = s["state"]
     lane = iota((1, LANES), 1)
     for t in range(height // 4):
-        letters = [inbox[16 * k + t].astype(f32) for k in range(4)]
+        letters = [inbox[t % 8, 2 * k + t // 8].astype(f32) for k in range(4)]
         for slab in range(3):
             x = letters[(3 - slab) % 4]
             for k in range(3):
@@ -589,7 +622,8 @@
     squares = fold(top[...] * top[...])
     total = jnp.sum(score, axis=0, keepdims=True) + jnp.sum(score_top, axis=0, keepdims=True)
     total = total - 0.5 * jnp.sum(squares, axis=0, keepdims=True)
-    lik_out[0] = (jnp.sum(total) + fixed) / (channels * cells)
+    total = jnp.sum(total, axis=1, keepdims=True)
+    lik_out[...] = jnp.broadcast_to((total + fixed) / (channels * cells), (8, LANES))
     turned = s["turned"]
     for v in range(4):
         turned[v * LANES : (v + 1) * LANES, :top_channels] = jnp.transpose(
@@ -616,21 +650,25 @@
         mid_out[img, 8:, :] = z[:4, width : 2 * width]
     for copy in z_copies:
         copy.wait_send()
-    pltpu.make_async_remote_copy(
-        src_ref=inbox.at[pl.ds(0, peers - 1)],
-        dst_ref=inbox.at[pl.ds(0, peers - 1)],
-        send_sem=send_sem,
-        recv_sem=recv_sem.at[0],
-        device_id=device(r, c),
-        device_id_type=MESH,
-    ).wait_send()
+    for ref, sem in (
+        (stage.at[pl.ds(0, n_rows - 1)], stage_send),
+        (inbox.at[pl.ds(0, n_chan - 1)], piece_send),
+    ):
+        pltpu.make_async_remote_copy(
+            src_ref=ref,
+            dst_ref=ref,
+            send_sem=sem,
+            recv_sem=hello_sem.at[0],
+            device_id=device(r, c),
+            device_id_type=MESH,
+        ).wait_send()
 
 
 def deliver(mid, top, lik, mid_out, top_out, lik_out):
     for img in range(mid.shape[0]):
         mid_out[img, :, 0, :] = mid[img]
     top_out[...] = top[...]
-    lik_out[0] = lik[0]
+    lik_out[...] = lik[0, :1]
 
 
 def body(sizes, images, *params):
@@ -647,7 +685,6 @@
     own = cells // 4 // n_rows
     operands = (images.reshape(n_imgs, channels, width),) + params
     vmem = pl.BlockSpec(memory_space=pltpu.VMEM)
-    smem = pl.BlockSpec(memory_space=pltpu.SMEM)
     count = len(operands)
     work = work_scratch(steps_mid, steps_top, hidden, channels, top_channels, cells)
     mid, top, lik = pl.pallas_call(
@@ -655,20 +692,24 @@
         out_shape=(
             pltpu.VMEM((n_imgs, half, width), f32),
             pltpu.VMEM((1, own, top_channels), f32),
-            jax.ShapeDtypeStruct((1,), f32),
+            pltpu.VMEM((8, LANES), f32),
         ),
         in_specs=[pl.BlockSpec(memory_space=pl.ANY)] * count,
-        out_specs=(vmem, vmem, smem),
+        out_specs=(vmem, vmem, vmem),
         scratch_shapes=[pltpu.VMEM(x.shape, x.dtype) for x in operands]
         + list(work.values())
         + [
             pltpu.VMEM((n_chan, 8, LANES), bf16),
-            pltpu.VMEM((peers, 8, LANES), bf16),
+            pltpu.VMEM((n_rows, n_chan, 8, LANES), bf16),
+            pltpu.VMEM((n_chan, n_rows, 8, LANES), bf16),
             pltpu.VMEM((n_chan, 8, LANES), f32),
             pltpu.VMEM((n_chan, 8, LANES), f32),
             pltpu.SemaphoreType.DMA((count,)),
             pltpu.SemaphoreType.DMA,
-            pltpu.SemaphoreType.DMA((peers,)),
+            pltpu.SemaphoreType.DMA,
+            pltpu.SemaphoreType.DMA((n_rows,)),
+            pltpu.SemaphoreType.DMA((n_chan,)),
+            pltpu.SemaphoreType.DMA((n_chan,)),
             pltpu.SemaphoreType.DMA((n_chan,)),
             pltpu.SemaphoreType.DMA((n_chan,)),
         ],
@@ -682,10 +723,10 @@
         out_shape=(
             jax.ShapeDtypeStruct((n_imgs, half, own_rows, width), f32),
             jax.ShapeDtypeStruct(top.shape, f32),
-            jax.ShapeDtypeStruct(lik.shape, f32),
+            jax.ShapeDtypeStruct((1,), f32),
         ),
-        in_specs=[vmem, vmem, smem],
-        out_specs=(vmem, vmem, smem),
+        in_specs=[vmem, vmem, vmem],
+        out_specs=(vmem, vmem, vmem),
         compiler_params=pltpu.CompilerParams(vmem_limit_bytes=4 * 1024 * 1024),
         name="deliver",
     )(mid, top, lik)

time: 39.5 us -> 46 us (1.16)
  the two profiles are of different devices: /device:TPU:205 before, /device:TPU:449 now
where the time goes in v3:
time: 46 us; the launch traced here: 45.9 us
  Pallas kernels  45.2 us (98%)
  between operations  0.65 us (1%)
    pallas_call x1, Pallas kernels, body(): pl.pallas_call(functools.partial(kernel, (n_rows, n_chan, height, width,...  44.6 us

profile of v3, /device:TPU:449, one launch (start us, length us, event | category | flops | bytes accessed | tf_op | source)
XLA Modules:
  0.0 45.9 jit_solution(13443507612798318225)
XLA Ops:
  0.6 44.6 %flow.1 = (f32[8,12,32]{2,1,0:T(8,128)S(1)}, f32[1,64,48]{2,1,0:T(8,128)S(1)}, f32[8,128]{1,0:T(8,128)S(1)}) custom-call(f32[8,24,32]{2,1,0:T(8,128)} %bitcast.14, f32[3,24]{1,0:T(4,128)} %refs_1_.1, f32[3,24]{1,0:T(4,128)} %refs_2_.1, f32[3,24,24]{2,1,0:T(8,128)} %refs_3_.1, f32[3,24,24]{2,1,0:T(8,128)} %refs_4_.1, f32[3,24]{1,0:T(4,128)} %refs_5_.1, ...), custom_call_target="tpu_custom_call" | custom-call | tf_op jit(solution)/shard_map/flow/pallas_call | solution.py:690
  45.2 0.7 %deliver.1 = (f32[8,12,1,32]{3,2,1,0:T(1,128)}, f32[1,64,48]{2,1,0:T(8,128)}, f32[1]{0:T(128)}) custom-call(f32[8,12,32]{2,1,0:T(8,128)S(1)} %get-tuple-element.9.mid, f32[1,64,48]{2,1,0:T(8,128)S(1)} %get-tuple-element.10.top, f32[8,128]{1,0:T(8,128)S(1)} %get-tuple-element.11.lik), custom_call_target="tpu_custom_call" | custom-call | tf_op jit(solution)/shard_map/deliver/pallas_call | solution.py:721

commit v4 on v3

--- a/solution.py
+++ b/solution.py
@@ -545,19 +545,29 @@
     fixed = fixed + cells // 4 * (jnp.sum(p["gain_top"][...]) + jnp.sum(p["diag_top"][...]))
     fixed = fixed - 0.5 * log_two_pi * channels * cells
 
+    for row in range(1, n_rows):
+
+        @pl.when(row > r)
+        def _():
+            await_copy(stage.at[row], stage_sem.at[row])
+            send_row(row)
+            for q in range(n_chan - 1):
+                pl.when(q < spot)(functools.partial(send_piece, row, q))
+
     for q in range(1, n_chan):
 
         @pl.when(q > spot)
         def _():
             await_copy(inbox.at[chans[q], 0], hello_sem.at[chans[q]])
             send_hello(q)
-
-    for row in range(n_rows):
-
-        @pl.when(row != r)
+            for row in range(1, n_rows):
+                pl.when(row > r)(functools.partial(send_piece, row, q))
+
+    for row in range(n_rows - 1):
+
+        @pl.when(row < r)
         def _():
             await_copy(stage.at[row], stage_sem.at[row])
-            pl.when(row > r)(functools.partial(send_row, row))
             for q in range(n_chan):
                 pl.when(q != spot)(functools.partial(send_piece, row, q))
 

time: 46 us -> 37.1 us (0.81)
  the two profiles are of different devices: /device:TPU:449 before, /device:TPU:1 now
where the time goes in v4:
time: 37.1 us; the launch traced here: 36.9 us
  Pallas kernels  36.3 us (98%)
  between operations  0.65 us (2%)
    pallas_call x1, Pallas kernels, body(): pl.pallas_call(functools.partial(kernel, (n_rows, n_chan, height, width,...  35.6 us

profile of v4, /device:TPU:1, one launch (start us, length us, event | category | flops | bytes accessed | tf_op | source)
XLA Modules:
  0.0 36.9 jit_solution(1405958215937994677)
XLA Ops:
  0.6 35.6 %flow.1 = (f32[8,12,32]{2,1,0:T(8,128)S(1)}, f32[1,64,48]{2,1,0:T(8,128)S(1)}, f32[8,128]{1,0:T(8,128)S(1)}) custom-call(f32[8,24,32]{2,1,0:T(8,128)} %bitcast.14, f32[3,24]{1,0:T(4,128)} %refs_1_.1, f32[3,24]{1,0:T(4,128)} %refs_2_.1, f32[3,24,24]{2,1,0:T(8,128)} %refs_3_.1, f32[3,24,24]{2,1,0:T(8,128)} %refs_4_.1, f32[3,24]{1,0:T(4,128)} %refs_5_.1, ...), custom_call_target="tpu_custom_call" | custom-call | tf_op jit(solution)/shard_map/flow/pallas_call | solution.py:700
  36.3 0.7 %deliver.1 = (f32[8,12,1,32]{3,2,1,0:T(1,128)}, f32[1,64,48]{2,1,0:T(8,128)}, f32[1]{0:T(128)}) custom-call(f32[8,12,32]{2,1,0:T(8,128)S(1)} %get-tuple-element.9.mid, f32[1,64,48]{2,1,0:T(8,128)S(1)} %get-tuple-element.10.top, f32[8,128]{1,0:T(8,128)S(1)} %get-tuple-element.11.lik), custom_call_target="tpu_custom_call" | custom-call | tf_op jit(solution)/shard_map/deliver/pallas_call | solution.py:731

commit v5 on v4

--- a/solution.py
+++ b/solution.py
@@ -91,6 +91,10 @@
     half = channels // 2
     mapping = mid_map(channels)
     natural = eye_map(top_channels)
+    for name in ("u", "y"):
+        shape = s[name].shape
+        for at in (0, shape[2] - LANES):
+            s[name][:, :, at : at + LANES] = jnp.zeros(shape[:2] + (LANES,), f32)
     for k in range(steps_mid):
         mat, bias = mixing(
             p["lower_mid"][k],
@@ -159,13 +163,6 @@
 
 def lane_of(n):
     return lax.rem(iota((1, n), 1), LANES)
-
-
-def edge_mid(x, dr):
-    lane = iota((1, LANES), 1)
-    if dr > 0:
-        return keep(roll(x, -32), lane < 96)
-    return keep(roll(x, 32), lane >= 32)
 
 
 def edge_top(x, dr):
@@ -245,75 +242,97 @@
     y_ref[:rows, lo : lo + n] = jnp.dot(third[...], h, preferred_element_type=f32)
 
 
-def mid_step(s, k, exact):
+def row_sum(y_ref, k, tap_rows, lo, hi):
+    total = None
+    n = hi - lo
+    for dc in (0, -1, 1):
+        base = 4 + dc
+        rows = slice(base * tap_rows, (base + 1) * tap_rows)
+        part = y_ref[k, rows, LANES + lo : LANES + hi]
+        rows = slice((base + 3) * tap_rows, (base + 4) * tap_rows)
+        part = part + roll(y_ref[k, rows, LANES + lo : 2 * LANES + hi], -32)[:, :n]
+        rows = slice((base - 3) * tap_rows, (base - 2) * tap_rows)
+        part = part + roll(y_ref[k, rows, lo : LANES + hi], 32)[:, LANES:]
+        if dc != 0:
+            part = shift_col(part, dc, 1)
+        total = part if total is None else total + part
+    return total
+
+
+def mid_step(s, k, exact, fresh, spread, done):
     state, u_ref, q_ref, y_ref = s["state"], s["u"], s["q"], s["y"]
-    channels, n = state.shape
-    block = 4 * LANES
+    channels = u_ref.shape[1]
     sub = iota((8, 1), 0)
     mat = s["mix_mid"][k, :, : (2 if exact else 3) * channels]
-    for lo in range(0, n, block):
-        u_ref[:, lo : lo + block] = mix(
-            mat, s["mix_bias_mid"][k], state[:, lo : lo + block], exact
-        )
-    for lo in range(0, n, block):
-        q = u_ref[:16, lo : lo + block]
-        q = jnp.concatenate([q[:8], jnp.where(sub == 4, 1.0, q[8:])], axis=0)
-        for dc in (-1, 0, 1):
-            x = q if dc == 0 else shift_col(q, dc, 1)
-            q_ref[dc + 1, :, LANES + lo : LANES + lo + block] = x.astype(bf16)
-            if lo == 0:
-                q_ref[dc + 1, :, LANES + n :] = edge_mid(x[:, :LANES], 1).astype(bf16)
-            if lo + block == n:
-                q_ref[dc + 1, :, :LANES] = edge_mid(x[:, block - LANES :], -1).astype(bf16)
-    for lo in range(0, n, min(CHUNK, n)):
-        taps = []
-        for dr in (-1, 0, 1):
-            at = lo + LANES * (1 + dr)
-            for dc in (-1, 0, 1):
-                taps.append(q_ref[dc + 1, :, at : at + min(CHUNK, n)])
-        product(
-            s["w1t_mid"].at[k],
-            s["w2t_mid"].at[k],
-            s["w3p_mid"].at[k],
-            s["b2_mid"].at[k],
-            jnp.concatenate(taps, axis=0),
-            y_ref,
-            9 * channels,
-            lo,
-        )
+    lo, hi = fresh[0] * LANES, fresh[1] * LANES
+    u_ref[k, :, LANES + lo : LANES + hi] = mix(
+        mat, s["mix_bias_mid"][k], state[k, :, lo:hi], exact
+    )
+    for lo in range(spread[0] * LANES, spread[1] * LANES, 2 * LANES):
+        hi = lo + 2 * LANES
+        rows = [
+            roll(u_ref[k, :16, lo : LANES + hi], 32)[:, LANES:],
+            u_ref[k, :16, LANES + lo : LANES + hi],
+            roll(u_ref[k, :16, LANES + lo : 2 * LANES + hi], -32)[:, : hi - lo],
+        ]
+        for dr in range(3):
+            for dc in range(3):
+                x = rows[dr]
+                if dr == 1 and dc == 1:
+                    x = jnp.concatenate([x[:8], jnp.where(sub == 4, 1.0, x[8:])], axis=0)
+                elif dc != 1:
+                    x = shift_col(x, dc - 1, 1)
+                tap = 3 * dr + dc
+                q_ref[16 * tap : 16 * tap + 16, lo:hi] = x.astype(bf16)
+    lo, hi = spread[0] * LANES, spread[1] * LANES
+    product(
+        s["w1t_mid"].at[k],
+        s["w2t_mid"].at[k],
+        s["w3p_mid"].at[k],
+        s["b2_mid"].at[k],
+        q_ref[:, lo:hi],
+        y_ref.at[k],
+        9 * channels,
+        LANES + lo,
+    )
     score = None
-    width = 2 * LANES
-    for lo in range(0, n, width):
-        out = gather(y_ref, channels, lo, lo + width, n, edge_mid, 1) + wide(s["b3_mid"][k], width)
+    for tile in range(done[0], done[1]):
+        lo, hi = tile * LANES, (tile + 1) * LANES
+        out = row_sum(y_ref, k, channels, lo, hi) + s["b3_mid"][k]
         gate, logs = gated(out[:16] + 2.0)
-        logs = fold(logs)
         score = logs if score is None else score + logs
-        u = u_ref[:, lo : lo + width]
-        state[:8, lo : lo + width] = u[:8]
+        u = u_ref[k, :, LANES + lo : LANES + hi]
+        state[k + 1, :8, lo:hi] = u[:8]
         late = (u[8:16] + out[8:16]) * pltpu.roll(gate[8:16], 4, 0)
-        state[8:16, lo : lo + width] = jnp.where(sub < 4, u[8:16], late)
-        state[16:, lo : lo + width] = (u[16:] + out[16:]) * gate[:8]
+        state[k + 1, 8:16, lo:hi] = jnp.where(sub < 4, u[8:16], late)
+        state[k + 1, 16:, lo:hi] = (u[16:] + out[16:]) * gate[:8]
     return keep(score, iota((16, 1), 0) < channels // 2)
 
 
-def squeeze(s):
-    state, top = s["state"], s["top"]
-    odd = lax.rem(iota((1, LANES), 1), 2) == 1
+def squeeze(state, top):
+    lane = iota((1, LANES), 1)
+    odd = lax.rem(lane, 2) == 1
+    block = lax.div(lane, 32)
     sub = iota((8, 1), 0)
     for v in range(4):
-        tails = []
         for i in range(2):
-            t = (2 * v + i) * LANES
-            a = state[8:, t : t + LANES]
-            t = t + 8 * LANES
-            b = state[8:, t : t + LANES]
-            even_col = jnp.where(odd, roll(b, 1), a)
-            odd_col = jnp.where(odd, b, roll(a, -1))
+            both = []
+            for j in range(2):
+                x = None
+                for b in range(4):
+                    tile = (4 * b + v // 2) * LANES
+                    shift = 32 * (b - 2 * (v % 2) - i) - j
+                    near = roll(state[8:, tile : tile + LANES], shift)
+                    tile = tile + 2 * LANES
+                    far = roll(state[8:, tile : tile + LANES], shift + 1)
+                    near = jnp.where(odd, far, near)
+                    x = near if x is None else jnp.where(block == b, near, x)
+                both.append(x)
             cols = slice(v * LANES, (v + 1) * LANES)
-            top[16 * i : 16 * i + 8, cols] = even_col[8:]
-            top[16 * i + 8 : 16 * i + 16, cols] = odd_col[8:]
+            top[16 * i : 16 * i + 8, cols] = both[0][8:]
+            top[16 * i + 8 : 16 * i + 16, cols] = both[1][8:]
             top[32 + 8 * i : 40 + 8 * i, cols] = jnp.where(
-                sub < 4, pltpu.roll(odd_col[:8], 4, 0), even_col[:8]
+                sub < 4, pltpu.roll(both[1][:8], 4, 0), both[0][:8]
             )
 
 
@@ -374,10 +393,10 @@
         "w1t_top": pltpu.VMEM((steps_top, hidden, 9 * top_channels // 2 + 8), bf16),
         "w2t_top": pltpu.VMEM((steps_top, hidden, hidden), bf16),
         "b2_top": pltpu.VMEM((steps_top, hidden, LANES), f32),
-        "state": pltpu.VMEM((channels, cells), f32),
-        "u": pltpu.VMEM((channels, cells), f32),
-        "q": pltpu.VMEM((3, 16, cells + 2 * LANES), bf16),
-        "y": pltpu.VMEM((9 * channels, cells), f32),
+        "state": pltpu.VMEM((steps_mid + 1, channels, cells), f32),
+        "u": pltpu.VMEM((steps_mid, channels, cells + 2 * LANES), f32),
+        "q": pltpu.VMEM((144, cells), bf16),
+        "y": pltpu.VMEM((steps_mid, 9 * channels, cells + 2 * LANES), f32),
         "top": pltpu.VMEM((top_channels, n_top), f32),
         "u_top": pltpu.VMEM((top_channels, n_top), f32),
         "q_top": pltpu.VMEM((3, top_channels // 2, n_top + 2 * LANES), f32),
@@ -478,7 +497,7 @@
     for dest in range(n_chan):
         x = images[dest]
         x = jnp.concatenate([x[:8], x[8:16], x[16:], jnp.zeros((8, width), f32)], axis=1)
-        outbox[dest] = pltpu.roll(x, quad * 32, 1).astype(bf16)
+        outbox[dest] = pltpu.roll(x, lax.rem(c, 4) * 32, 1).astype(bf16)
 
     @pl.when(r + spot > 0)
     def _():
@@ -509,7 +528,7 @@
             src_ref=stage.at[row, chans[q]],
             dst_ref=inbox.at[c, row],
             send_sem=piece_send,
-            recv_sem=piece_sem.at[c],
+            recv_sem=piece_sem.at[row // 4, c],
             device_id=device(r, chans[q]),
             device_id_type=MESH,
         ).start()
@@ -573,57 +592,70 @@
 
     for row in range(n_rows):
         inbox[c, row] = stage[row, c]
-    for q in range(n_chan):
-
-        @pl.when(q < spot)
-        def _():
-            await_copy(inbox.at[chans[q], 0], hello_sem.at[chans[q]])
-
-        @pl.when(q != spot)
-        def _():
-            await_copy(inbox.at[chans[q], pl.ds(0, n_rows - 1)], piece_sem.at[chans[q]])
-
     state = s["state"]
     lane = iota((1, LANES), 1)
-    for t in range(height // 4):
-        letters = [inbox[t % 8, 2 * k + t // 8].astype(f32) for k in range(4)]
-        for slab in range(3):
-            x = letters[(3 - slab) % 4]
-            for k in range(3):
-                x = jnp.where(lax.div(lane, 32) == k, letters[(k - slab) % 4], x)
-            state[8 * slab : 8 * slab + 8, t * LANES : (t + 1) * LANES] = roll(x, -32 * slab)
-
-    score = None
-    for k in range(p["shift_mid"].shape[0]):
-        logs = mid_step(s, k, k == 0)
-        score = logs if score is None else score + logs
-
-    for to in range(n_chan):
-        start = pl.multiple_of((side * n_chan + to) * LANES, LANES)
-        z = state[:16, pl.ds(start, LANES)]
-        z_send[to] = jnp.where(
-            lane < 32,
-            pltpu.roll(z[:8], LANES - quad * 32, 1),
-            pltpu.roll(z[8:], LANES + 32 - quad * 32, 1),
-        )
-    z_copies = []
-    for d in range(1, n_chan):
-        other = lax.rem(c + d, n_chan)
-        copy = pltpu.make_async_remote_copy(
-            src_ref=z_send.at[other],
-            dst_ref=z_recv.at[c],
-            send_sem=z_send_sem.at[d],
-            recv_sem=z_recv_sem.at[d],
-            device_id=device(r, other),
-            device_id_type=MESH,
-        )
-        copy.start()
-        z_copies.append(copy)
-    z_recv[c] = z_send[c]
-
-    squares = fold(state[:16, :] * state[:16, :])
+    upper = n_rows // 2
+
+    def collect(part):
+        for q in range(n_chan):
+
+            @pl.when((q < spot) & (lax.div(r, upper) == part))
+            def _():
+                await_copy(inbox.at[chans[q], 0], hello_sem.at[chans[q]])
+
+            for own, pieces in ((part, upper - 1), (1 - part, upper)):
+
+                @pl.when((q != spot) & (lax.div(r, upper) == own))
+                def _():
+                    await_copy(
+                        inbox.at[chans[q], pl.ds(upper * part, pieces)],
+                        piece_sem.at[part, chans[q]],
+                    )
+
+        for t in range(2 * upper * part, 2 * upper * (part + 1)):
+            letters = [inbox[4 * (t % 2) + k, t // 2].astype(f32) for k in range(4)]
+            for slab in range(3):
+                x = letters[(3 - slab) % 4]
+                for k in range(3):
+                    x = jnp.where(lax.div(lane, 32) == k, letters[(k - slab) % 4], x)
+                x = roll(x, -32 * slab)
+                state[0, 8 * slab : 8 * slab + 8, t * LANES : (t + 1) * LANES] = x
+
+    def send_latent():
+        start = pl.multiple_of(2 * r * LANES, LANES)
+        for to in range(n_chan):
+            z = state[3, :16, pl.ds(start + to // 4 * LANES, LANES)]
+            shift = -32 * (to % 4)
+            z_send[to] = jnp.where(lane < 32, roll(z[:8], shift), roll(z[8:], shift + 32))
+        for q in range(n_chan):
+
+            @pl.when(q != spot)
+            def _():
+                pltpu.make_async_remote_copy(
+                    src_ref=z_send.at[chans[q]],
+                    dst_ref=z_recv.at[c],
+                    send_sem=z_send_sem,
+                    recv_sem=z_recv_sem.at[c],
+                    device_id=device(r, chans[q]),
+                    device_id_type=MESH,
+                ).start()
+
+        z_recv[c] = z_send[c]
+
+    collect(0)
+    score = mid_step(s, 0, True, (0, 8), (0, 8), (0, 7))
+    score = score + mid_step(s, 1, False, (0, 7), (0, 8), (0, 6))
+    score = score + mid_step(s, 2, False, (0, 6), (0, 6), (0, 5))
+    pl.when(r < 2)(send_latent)
+    collect(1)
+    score = score + mid_step(s, 0, True, (8, 16), (6, 16), (7, 16))
+    score = score + mid_step(s, 1, False, (7, 16), (6, 16), (6, 16))
+    score = score + mid_step(s, 2, False, (6, 16), (4, 16), (5, 16))
+    pl.when(r >= 2)(send_latent)
+
+    squares = fold(state[3, :16, :] * state[3, :16, :])
     score = score - 0.5 * keep(squares, iota((16, 1), 0) < half)
-    squeeze(s)
+    squeeze(state.at[3], s["top"])
     score_top = None
     for k in range(p["shift_top"].shape[0]):
         logs = top_step(s, k)
@@ -645,24 +677,20 @@
             :, :top_channels
         ]
 
-    for d in range(1, n_chan):
-        pltpu.make_async_remote_copy(
-            src_ref=z_send.at[0],
-            dst_ref=z_recv.at[lax.rem(c + n_chan - d, n_chan)],
-            send_sem=z_send_sem.at[d],
-            recv_sem=z_recv_sem.at[d],
-            device_id=device(r, c),
-            device_id_type=MESH,
-        ).wait_recv()
+    for q in range(n_chan):
+
+        @pl.when(q != spot)
+        def _():
+            await_copy(z_recv.at[chans[q]], z_recv_sem.at[chans[q]])
+
     for img in range(n_chan):
         z = z_recv[img]
         mid_out[img, :8, :] = z[:, :width]
         mid_out[img, 8:, :] = z[:4, width : 2 * width]
-    for copy in z_copies:
-        copy.wait_send()
     for ref, sem in (
         (stage.at[pl.ds(0, n_rows - 1)], stage_send),
         (inbox.at[pl.ds(0, n_chan - 1)], piece_send),
+        (z_recv.at[pl.ds(0, n_chan - 1)], z_send_sem),
     ):
         pltpu.make_async_remote_copy(
             src_ref=ref,
@@ -719,8 +747,8 @@
             pltpu.SemaphoreType.DMA,
             pltpu.SemaphoreType.DMA((n_rows,)),
             pltpu.SemaphoreType.DMA((n_chan,)),
-            pltpu.SemaphoreType.DMA((n_chan,)),
-            pltpu.SemaphoreType.DMA((n_chan,)),
+            pltpu.SemaphoreType.DMA((2, n_chan)),
+            pltpu.SemaphoreType.DMA,
             pltpu.SemaphoreType.DMA((n_chan,)),
         ],
         compiler_params=pltpu.CompilerParams(

time: 37.1 us -> 38.1 us (1.027)
  the two profiles are of different devices: /device:TPU:1 before, /device:TPU:132 now
where the time goes in v5:
time: 38.1 us; the launch traced here: 38 us
  Pallas kernels  37.3 us (98%)
  between operations  0.65 us (2%)
    pallas_call x1, Pallas kernels, body(): pl.pallas_call(functools.partial(kernel, (n_rows, n_chan, height, width,...  36.7 us

profile of v5, /device:TPU:132, one launch (start us, length us, event | category | flops | bytes accessed | tf_op | source)
XLA Modules:
  0.0 38.0 jit_solution(7218587991824582668)
XLA Ops:
  0.6 36.7 %flow.1 = (f32[8,12,32]{2,1,0:T(8,128)S(1)}, f32[1,64,48]{2,1,0:T(8,128)S(1)}, f32[8,128]{1,0:T(8,128)S(1)}) custom-call(f32[8,24,32]{2,1,0:T(8,128)} %bitcast.14, f32[3,24]{1,0:T(4,128)} %refs_1_.1, f32[3,24]{1,0:T(4,128)} %refs_2_.1, f32[3,24,24]{2,1,0:T(8,128)} %refs_3_.1, f32[3,24,24]{2,1,0:T(8,128)} %refs_4_.1, f32[3,24]{1,0:T(4,128)} %refs_5_.1, ...), custom_call_target="tpu_custom_call" | custom-call | tf_op jit(solution)/shard_map/flow/pallas_call | solution.py:728
  37.3 0.7 %deliver.1 = (f32[8,12,1,32]{3,2,1,0:T(1,128)}, f32[1,64,48]{2,1,0:T(8,128)}, f32[1]{0:T(128)}) custom-call(f32[8,12,32]{2,1,0:T(8,128)S(1)} %get-tuple-element.9.mid, f32[1,64,48]{2,1,0:T(8,128)S(1)} %get-tuple-element.10.top, f32[8,128]{1,0:T(8,128)S(1)} %get-tuple-element.11.lik), custom_call_target="tpu_custom_call" | custom-call | tf_op jit(solution)/shard_map/deliver/pallas_call | solution.py:759

commit v6 on v4

--- a/solution.py
+++ b/solution.py
@@ -245,7 +245,7 @@
     y_ref[:rows, lo : lo + n] = jnp.dot(third[...], h, preferred_element_type=f32)
 
 
-def mid_step(s, k, exact):
+def mid_step(s, k, exact, mixed=None):
     state, u_ref, q_ref, y_ref = s["state"], s["u"], s["q"], s["y"]
     channels, n = state.shape
     block = 4 * LANES
@@ -255,6 +255,8 @@
         u_ref[:, lo : lo + block] = mix(
             mat, s["mix_bias_mid"][k], state[:, lo : lo + block], exact
         )
+    if mixed is not None:
+        mixed()
     for lo in range(0, n, block):
         q = u_ref[:16, lo : lo + block]
         q = jnp.concatenate([q[:8], jnp.where(sub == 4, 1.0, q[8:])], axis=0)
@@ -593,33 +595,36 @@
                 x = jnp.where(lax.div(lane, 32) == k, letters[(k - slab) % 4], x)
             state[8 * slab : 8 * slab + 8, t * LANES : (t + 1) * LANES] = roll(x, -32 * slab)
 
+    z_copies = []
+
+    def send_latent():
+        for to in range(n_chan):
+            start = pl.multiple_of((side * n_chan + to) * LANES, LANES)
+            z = s["u"][:16, pl.ds(start, LANES)]
+            z_send[to] = jnp.where(
+                lane < 32,
+                pltpu.roll(z[:8], LANES - quad * 32, 1),
+                pltpu.roll(z[8:], LANES + 32 - quad * 32, 1),
+            )
+        for d in range(1, n_chan):
+            other = lax.rem(c + d, n_chan)
+            copy = pltpu.make_async_remote_copy(
+                src_ref=z_send.at[other],
+                dst_ref=z_recv.at[c],
+                send_sem=z_send_sem.at[d],
+                recv_sem=z_recv_sem.at[d],
+                device_id=device(r, other),
+                device_id_type=MESH,
+            )
+            copy.start()
+            z_copies.append(copy)
+        z_recv[c] = z_send[c]
+
     score = None
-    for k in range(p["shift_mid"].shape[0]):
-        logs = mid_step(s, k, k == 0)
+    last = p["shift_mid"].shape[0] - 1
+    for k in range(last + 1):
+        logs = mid_step(s, k, k == 0, send_latent if k == last else None)
         score = logs if score is None else score + logs
-
-    for to in range(n_chan):
-        start = pl.multiple_of((side * n_chan + to) * LANES, LANES)
-        z = state[:16, pl.ds(start, LANES)]
-        z_send[to] = jnp.where(
-            lane < 32,
-            pltpu.roll(z[:8], LANES - quad * 32, 1),
-            pltpu.roll(z[8:], LANES + 32 - quad * 32, 1),
-        )
-    z_copies = []
-    for d in range(1, n_chan):
-        other = lax.rem(c + d, n_chan)
-        copy = pltpu.make_async_remote_copy(
-            src_ref=z_send.at[other],
-            dst_ref=z_recv.at[c],
-            send_sem=z_send_sem.at[d],
-            recv_sem=z_recv_sem.at[d],
-            device_id=device(r, other),
-            device_id_type=MESH,
-        )
-        copy.start()
-        z_copies.append(copy)
-    z_recv[c] = z_send[c]
 
     squares = fold(state[:16, :] * state[:16, :])
     score = score - 0.5 * keep(squares, iota((16, 1), 0) < half)

time: 37.1 us -> 35.6 us (0.960)
  Pallas kernels: 36.3 us -> 34.8 us
    pallas_call x1, Pallas kernels: 35.6 us -> 34.2 us  [body(): pl.pallas_call(functools.partial(kernel, (n_rows, n_chan, height, width,...]
where the time goes in v6:
time: 35.6 us; the launch traced here: 35.5 us
  Pallas kernels  34.8 us (98%)
  between operations  0.65 us (2%)
    pallas_call x1, Pallas kernels, body(): pl.pallas_call(functools.partial(kernel, (n_rows, n_chan, height, width,...  34.2 us

profile of v6, /device:TPU:1, one launch (start us, length us, event | category | flops | bytes accessed | tf_op | source)
XLA Modules:
  0.0 35.5 jit_solution(5290981183158182315)
XLA Ops:
  0.6 34.2 %flow.1 = (f32[8,12,32]{2,1,0:T(8,128)S(1)}, f32[1,64,48]{2,1,0:T(8,128)S(1)}, f32[8,128]{1,0:T(8,128)S(1)}) custom-call(f32[8,24,32]{2,1,0:T(8,128)} %bitcast.14, f32[3,24]{1,0:T(4,128)} %refs_1_.1, f32[3,24]{1,0:T(4,128)} %refs_2_.1, f32[3,24,24]{2,1,0:T(8,128)} %refs_3_.1, f32[3,24,24]{2,1,0:T(8,128)} %refs_4_.1, f32[3,24]{1,0:T(4,128)} %refs_5_.1, ...), custom_call_target="tpu_custom_call" | custom-call | tf_op jit(solution)/shard_map/flow/pallas_call | solution.py:705
  34.8 0.7 %deliver.1 = (f32[8,12,1,32]{3,2,1,0:T(1,128)}, f32[1,64,48]{2,1,0:T(8,128)}, f32[1]{0:T(128)}) custom-call(f32[8,12,32]{2,1,0:T(8,128)S(1)} %get-tuple-element.9.mid, f32[1,64,48]{2,1,0:T(8,128)S(1)} %get-tuple-element.10.top, f32[8,128]{1,0:T(8,128)S(1)} %get-tuple-element.11.lik), custom_call_target="tpu_custom_call" | custom-call | tf_op jit(solution)/shard_map/deliver/pallas_call | solution.py:736

commit v7 on v6

--- a/solution.py
+++ b/solution.py
@@ -526,8 +526,7 @@
             device_id_type=MESH,
         ).wait_recv()
 
-    for row in range(n_rows - 1):
-        pl.when(row < r)(functools.partial(send_row, row))
+    pl.when(r > 0)(functools.partial(send_row, 0))
     for q in range(n_chan - 1):
         pl.when(q < spot)(functools.partial(send_hello, q))
     copies = []
@@ -536,7 +535,10 @@
         copy.start()
         copies.append(copy)
     stage[r] = outbox[...]
-    for copy in copies:
+    copies[0].wait()
+    for row in range(1, n_rows - 1):
+        pl.when(row < r)(functools.partial(send_row, row))
+    for copy in copies[1:]:
         copy.wait()
     prepare(p, s)
     channels = p["shift_mid"].shape[1]

time: 35.6 us -> 35.5 us (level)
  no operation moved by 1% of the time
where the time goes in v7:
time: 35.5 us; the launch traced here: 35.4 us
  Pallas kernels  34.7 us (98%)
  between operations  0.65 us (2%)
    pallas_call x1, Pallas kernels, body(): pl.pallas_call(functools.partial(kernel, (n_rows, n_chan, height, width,...  34.1 us

profile of v7, /device:TPU:1, one launch (start us, length us, event | category | flops | bytes accessed | tf_op | source)
XLA Modules:
  0.0 35.4 jit_solution(15739486261649106586)
XLA Ops:
  0.6 34.1 %flow.1 = (f32[8,12,32]{2,1,0:T(8,128)S(1)}, f32[1,64,48]{2,1,0:T(8,128)S(1)}, f32[8,128]{1,0:T(8,128)S(1)}) custom-call(f32[8,24,32]{2,1,0:T(8,128)} %bitcast.14, f32[3,24]{1,0:T(4,128)} %refs_1_.1, f32[3,24]{1,0:T(4,128)} %refs_2_.1, f32[3,24,24]{2,1,0:T(8,128)} %refs_3_.1, f32[3,24,24]{2,1,0:T(8,128)} %refs_4_.1, f32[3,24]{1,0:T(4,128)} %refs_5_.1, ...), custom_call_target="tpu_custom_call" | custom-call | tf_op jit(solution)/shard_map/flow/pallas_call | solution.py:707
  34.7 0.7 %deliver.1 = (f32[8,12,1,32]{3,2,1,0:T(1,128)}, f32[1,64,48]{2,1,0:T(8,128)}, f32[1]{0:T(128)}) custom-call(f32[8,12,32]{2,1,0:T(8,128)S(1)} %get-tuple-element.9.mid, f32[1,64,48]{2,1,0:T(8,128)S(1)} %get-tuple-element.10.top, f32[8,128]{1,0:T(8,128)S(1)} %get-tuple-element.11.lik), custom_call_target="tpu_custom_call" | custom-call | tf_op jit(solution)/shard_map/deliver/pallas_call | solution.py:738
